TPU v7x, 128 devices: a whole 4x4x4 slice. The times are simulated.
128 devices in a mesh: dp: 1, ep: 64 (over z, y, x), tp: 2 (over core).
Axes of the slice: x: 4, y: 4, z: 4, core: 2. Of those that a mesh axis runs over, the one named last changes fastest.
Arguments:
- X: bfloat16 [32768, 2048], P(('dp', 'ep', 'tp'))
- idx: int32 [32768, 8], P(('dp', 'ep', 'tp'))
- g: float32 [32768, 8], P(('dp', 'ep', 'tp'))
- W1: bfloat16 [64, 2048, 1024], P('ep', None, 'tp')
- W3: bfloat16 [64, 2048, 1024], P('ep', None, 'tp')
- W2: bfloat16 [64, 1024, 2048], P('ep', 'tp')
Outputs:
- output: bfloat16 [32768, 2048], P(('dp', 'ep', 'tp'))
All inputs are finite; a program needn't handle non-finite values.
Results may differ from a plain program's by a relative error of at most 0.0107182.
Values are sent between devices in bfloat16 or wider.
A program may use at most 1 GiB of HBM per device.

v0:
```python
import jax
import jax.numpy as jnp
from jax import lax
from jax.sharding import PartitionSpec as P

CF = 2


def _route(idx, n_exp, cap):
    ids = idx.reshape(-1)
    oh = (ids[:, None] == jnp.arange(n_exp, dtype=jnp.int32)[None, :]).astype(jnp.int32)
    s = jnp.sum(oh * (jnp.cumsum(oh, axis=0) - 1), axis=1)
    keep = s < cap
    return jnp.where(keep, ids * cap + s, n_exp * cap), keep


def solution(mesh):
    ep, tp = mesh.shape["ep"], mesh.shape["tp"]
    rows = P(("dp", "ep", "tp"), None)

    def local(x, idx, g, w1, w3, w2):
        t_loc, d = x.shape
        top = idx.shape[1]
        el = w1.shape[0]
        n_exp = el * ep
        cap = CF * top * t_loc // n_exp
        dest, keep = _route(idx, n_exp, cap)
        xr = jnp.repeat(x, top, axis=0)
        buf = jnp.zeros((n_exp * cap, d), x.dtype).at[dest].set(xr, mode="drop").reshape(ep, el, cap, d)
        recv = lax.all_to_all(buf, "ep", 0, 0, tiled=True)
        allr = lax.all_gather(recv, "tp", axis=0)
        xe = allr.transpose(2, 0, 1, 3, 4).reshape(el, tp * ep * cap, d)
        h1 = jnp.einsum("erd,edf->erf", xe, w1, preferred_element_type=jnp.float32)
        h3 = jnp.einsum("erd,edf->erf", xe, w3, preferred_element_type=jnp.float32)
        h = (jax.nn.silu(h1) * h3).astype(jnp.bfloat16)
        yp = jnp.einsum("erf,efd->erd", h, w2, preferred_element_type=jnp.float32).astype(jnp.bfloat16)
        yp = yp.reshape(el, tp, ep, cap, d).transpose(1, 2, 0, 3, 4)
        parts = lax.all_to_all(yp, "tp", 0, 0, tiled=True)
        y = jnp.sum(parts.astype(jnp.float32), axis=0).astype(jnp.bfloat16)
        back = lax.all_to_all(y, "ep", 0, 0, tiled=True).reshape(n_exp * cap, d)
        ysel = back[jnp.minimum(dest, n_exp * cap - 1)].astype(jnp.float32).reshape(t_loc, top, d)
        wgt = jnp.where(keep, g.reshape(-1), 0.0).reshape(t_loc, top, 1)
        return jnp.sum(ysel * wgt, axis=1).astype(jnp.bfloat16)

    return jax.shard_map(local, mesh=mesh,
                         in_specs=(rows, rows, rows, P("ep", None, "tp"), P("ep", None, "tp"), P("ep", "tp", None)),
                         out_specs=rows, check_vma=False)
```

profile of v0, /device:TPU:0, one launch (start us, length us, event | category | flops | bytes accessed | tf_op | source)
XLA Modules:
  0.0 823.2 jit_solution(2475825165333211392)
XLA Ops:
  6.5 0.0 copy-start
  6.5 0.0 all-gather.3.cloned.1.call-start
  6.5 1.0 copy.14
  7.5 0.1 eq.29
  7.6 0.1 eq.25
  7.7 0.7 broadcast_multiply_fusion
  8.5 18.1 %reduce-window.6 = s32[64,16,128]{2,1,0:T(8,128)S(1)} reduce-window(s32[64,16,128]{2,1,0:T(8,128)S(1)} %fusion.12, s32[]{:T(128)} %constant.9.clone.1), window={size=1x1x128 pad=0_0x0_0x127_0}, to_apply=%region_0.0 | reduce-window | flops 16646144 | bytes 1048580 | tf_op jit(solution)/shard_map/reduce-window
  26.6 0.2 slice.10
  26.8 0.4 copy.21
  27.3 0.2 reduce-window.9
  27.5 0.2 add_add_fusion
  27.7 0.1 copy.18
  27.8 0.1 mul.39
  27.9 0.2 fusion.11
  28.1 0.0 copy-start.2
  28.1 0.6 copy-done.2
  28.7 0.6 compare_select_fusion
  29.3 21.9 %scatter_custom_fusion = bf16[4096,2048]{1,0:T(8,128)(2,1)} fusion(s32[2048]{0:T(1024)S(1)} %bitcast.57, bf16[]{:T(256)} %constant.8.clone.1, bf16[256,2048]{1,0:T(8,128)(2,1)} %param.6), kind=kCustom, calls=%fused_computation.6 | custom fusion | bytes 17825794 | tf_op jit(solution)/shard_map/scatter | solution.py:29
  51.2 226.3 %all_to_all.15 = bf16[64,1,64,2048]{3,2,1,0:T(8,128)(2,1)} all-to-all(bf16[64,1,64,2048]{3,2,1,0:T(8,128)(2,1)} %bitcast.49), channel_id=1, replica_groups=mesh['dp'=1,'ep'=64,'tp'=2] {'ep'}, dimensions={0} | all-to-all | bytes 33554432 | tf_op jit(solution)/shard_map/all_to_all | solution.py:30
  277.5 0.0 all-gather.3.cloned.1.call-update
  277.5 57.6 %all-gather.3.cloned.1.call-done = bf16[128,1,64,2048]{3,2,1,0:T(8,128)(2,1)} async-done(((bf16[64,1,64,2048]{3,2,1,0:T(8,128)(2,1)}), bf16[128,1,64,2048]{3,2,1,0:T(8,128)(2,1)}) %all-gather.3.cloned.1.call-update) | async-done | bytes 33554448 | tf_op jit(solution)/shard_map/all_gather | solution.py:31
  335.1 25.4 %fusion.8 = f32[8192,512]{1,0:T(8,128)} fusion(bf16[8192,2048]{1,0:T(8,128)(2,1)} %bitcast.58, bf16[1,2048,512]{2,1,0:T(8,128)(2,1)} %param.9), kind=kOutput, calls=%fused_computation.12 | convolution fusion | flops 17179869184 | bytes 52428800 | tf_op jit(solution)/shard_map/erd,edf->erf/dot_general | solution.py:33
  360.5 0.0 copy-done
  360.5 44.6 %convolution_convert_fusion = bf16[8192,2048]{1,0:T(8,128)(2,1)} fusion(f32[8192,512]{1,0:T(8,128)} %fusion.8, bf16[8192,2048]{1,0:T(8,128)(2,1)} %bitcast.59, bf16[1,512,2048]{2,1,0:T(8,128)(2,1)S(1)} %copy-done, bf16[1,2048,512]{2,1,0:T(8,128)(2,1)} %param.10), kind=kOutput, calls=%fused_computation.2 | convolution fusion | flops 34401681408 | bytes 88080384 | tf_op jit(solution)/shard_map/erf,efd->erd/dot_general | solution.py:36
  405.1 69.4 %all_to_all.16 = bf16[2,64,1,64,2048]{4,3,1,2,0:T(8,128)(2,1)} all-to-all(bf16[2,64,1,64,2048]{4,3,1,2,0:T(8,128)(2,1)} %bitcast.51), channel_id=1, replica_groups=mesh['dp'=1,'ep'=64,'tp'=2] {'tp'}, dimensions={0} | all-to-all | bytes 67108864 | tf_op jit(solution)/shard_map/all_to_all | solution.py:38
  474.5 20.8 %reduce_sum.36 = bf16[64,64,2048]{2,1,0:T(8,128)(2,1)} reduce(bf16[2,64,1,64,2048]{4,3,1,2,0:T(8,128)(2,1)} %all_to_all.16, bf16[]{:T(256)} %constant.8.clone.1), dimensions={0,2}, to_apply=%region_4.5 | reduce | flops 8388608 | bytes 50331648 | tf_op jit(solution)/shard_map/reduce_sum | solution.py:39
  495.4 0.0 copy-start.3
  495.4 0.0 copy-start.5
  495.4 0.0 copy-start.4
  495.4 10.8 %all-to-all-start.2 = ((bf16[64,1,64,2048]{3,2,1,0:T(8,128)(2,1)}), bf16[64,1,64,2048]{3,2,1,0:T(8,128)(2,1)}, u32[]{:S(2)}, u32[]{:S(2)}) async-start(bf16[64,1,64,2048]{3,2,1,0:T(8,128)(2,1)} %bitcast.50), calls=%async_computation.2 | async-start | bytes 33554432 | tf_op jit(solution)/shard_map/all_to_all | solution.py:40
  506.2 0.0 copy-done.3
  506.2 0.1 lt.45
  506.3 0.0 copy-done.5
  506.3 0.1 copy.20
  506.5 0.0 copy-done.4
  506.5 273.0 %all-to-all-done.2 = bf16[64,1,64,2048]{3,2,1,0:T(8,128)(2,1)} async-done(((bf16[64,1,64,2048]{3,2,1,0:T(8,128)(2,1)}), bf16[64,1,64,2048]{3,2,1,0:T(8,128)(2,1)}, u32[]{:S(2)}, u32[]{:S(2)}) %all-to-all-start.2) | async-done | bytes 16777248 | tf_op jit(solution)/shard_map/all_to_all | solution.py:40
  779.5 0.0 copy-start.1
  779.5 24.4 %gather_fusion = bf16[2048,2048]{1,0:T(8,128)(2,1)} fusion(bf16[4096,2048]{1,0:T(8,128)(2,1)} %bitcast.14, s32[2048]{0:T(1024)S(1)} %broadcast_clamp_fusion), kind=kCustom, calls=%fused_computation | custom fusion | bytes 16785408 | tf_op jit(solution)/shard_map/gather | solution.py:41
  803.9 12.2 %fusion = bf16[256,2048]{1,0:T(8,128)(2,1)} fusion(bf16[2048,2048]{1,0:T(8,128)(2,1)} %gather_fusion, f32[256,8]{1,0:T(8,128)S(1)} %broadcast_select_fusion), kind=kLoop, calls=%fused_computation.4 | loop fusion | flops 12058624 | bytes 9445376 | tf_op jit(solution)/shard_map/reduce_sum | solution.py:43
  816.1 0.0 copy-done.1
  (5 shorter events, 0.1 us)
Async XLA Ops:
  6.5 354.0 %copy-start = (bf16[1,512,2048]{2,1,0:T(8,128)(2,1)S(1)}, bf16[1,512,2048]{2,1,0:T(8,128)(2,1)}, u32[]{:S(2)}) copy-start(bf16[1,512,2048]{2,1,0:T(8,128)(2,1)} %param.11) | copy-start | bytes 6291460
  6.5 328.6 %all-gather.3.cloned.1.call-start = ((), (), s32[]{:S(2)}) async-start(), calls=%async_computation.3 | async-start | bytes 50331648 | tf_op jit(solution)/shard_map/all_gather | solution.py:31
  28.1 0.6 copy-start.2
  495.4 10.8 %copy-start.3 = (s32[2048]{0:T(1024)S(1)}, s32[2048]{0:T(1024)}, u32[]{:S(2)}) copy-start(s32[2048]{0:T(1024)} %copy-done.2) | copy-start | bytes 24580
  495.4 10.9 %copy-start.5 = (f32[256,8]{0,1:T(8,128)S(1)}, f32[256,8]{0,1:T(8,128)}, u32[]{:S(2)}) copy-start(f32[256,8]{0,1:T(8,128)} %param.8) | copy-start | bytes 24580
  495.4 11.1 %copy-start.4 = (s32[2048,1]{0,1:T(1,128)S(1)}, s32[2048,1]{0,1:T(1,128)}, u32[]{:S(2)}) copy-start(s32[2048,1]{0,1:T(1,128)} %get-tuple-element.5) | copy-start | bytes 24580
  495.4 284.1 %all-to-all-start.2 = ((bf16[64,1,64,2048]{3,2,1,0:T(8,128)(2,1)}), bf16[64,1,64,2048]{3,2,1,0:T(8,128)(2,1)}, u32[]{:S(2)}, u32[]{:S(2)}) async-start(bf16[64,1,64,2048]{3,2,1,0:T(8,128)(2,1)} %bitcast.50), calls=%async_computation.2 | async-start | bytes 33554432 | tf_op jit(solution)/shard_map/all_to_all | solution.py:40
  779.5 36.6 %copy-start.1 = (bf16[1,512,2048]{2,1,0:T(8,128)(2,1)S(1)}, bf16[1,512,2048]{2,1,0:T(8,128)(2,1)}, u32[]{:S(2)}) copy-start(bf16[1,512,2048]{2,1,0:T(8,128)(2,1)} %param.11) | copy-start | bytes 6291460
Sparse Core Ops, SparseCore 0:
  277.7 57.4 all-gather.2
where the time goes:
time: 836 us; the launch traced here: 823 us
  waiting for transfers between devices  331 us (40%)
  blocking collectives  296 us (35%)
  matrix products  70 us (8%)
  other arithmetic  53.2 us (6%)
  local copies, waits for them, and re-layouts  49.2 us (6%)
  between operations  13.7 us (2%)
  starting transfers between devices  10.8 us (1%)
    all_to_all x1, waiting for transfers between devices, local(): back = lax.all_to_all(y, 'ep', 0, 0, tiled=True).reshape(n_exp * cap, d)  273 us
    all_to_all x1, blocking collectives, local(): recv = lax.all_to_all(buf, 'ep', 0, 0, tiled=True)  226 us
    all_to_all x1, blocking collectives, local(): parts = lax.all_to_all(yp, 'tp', 0, 0, tiled=True)  69.4 us
    all_gather x1, waiting for transfers between devices, local(): allr = lax.all_gather(recv, 'tp', axis=0)  57.6 us
    dot_general x1, matrix products, local(): jnp.einsum('erf,efd->erd', h, w2, preferred_element_type=jnp.float32)  44.6 us
    dot_general x1, matrix products, local(): h1 = jnp.einsum('erd,edf->erf', xe, w1, preferred_element_type=jnp.float32)  25.4 us
    gather x1, local copies, waits for them, and re-layouts, local(): back[jnp.minimum(dest, n_exp * cap - 1)].astype(jnp.float32)  24.4 us
    scatter x1, local copies, waits for them, and re-layouts, local(): jnp.zeros((n_exp * cap, d), x.dtype).at[dest].set(xr, mode='drop')  21.9 us
  transfers between devices with their start and end apart: 2, of which 2 were waited for; matrix products, arithmetic and copies ran while one was open for 0% of the time, Pallas kernels for 0%

commit v1 on v0

v1 whole, which is shorter than its diff:
```python
import functools

import jax
import jax.numpy as jnp
from jax import lax
from jax.experimental import pallas as pl
from jax.experimental.pallas import tpu as pltpu
from jax.sharding import PartitionSpec as P

CF = 2
N_AX = 4
AXES = 3
VMEM_LIMIT = 60 * 2**20
MESH = pl.DeviceIdType.MESH
BF = jnp.bfloat16
F32 = jnp.float32


def _coords(me):
    return [(me // N_AX**a) % N_AX for a in range(AXES)]


def _shift(m, moves):
    return sum(((m[a] + moves.get(a, 0)) % N_AX) * N_AX**a for a in range(AXES))


def _color(c):
    return (c + 1) % 3, (c + 2) % 3, c


def _barrier(m, tp):
    bar = pltpu.get_barrier_semaphore()
    for a in range(AXES):
        for d in range(1, N_AX):
            pl.semaphore_signal(bar, inc=1, device_id={"ep": _shift(m, {a: d})}, device_id_type=MESH)
    pl.semaphore_signal(bar, inc=1, device_id={"tp": 1 - tp}, device_id_type=MESH)
    pl.semaphore_wait(bar, AXES * (N_AX - 1) + 1)


def _order(k):
    return 1 + 2 * k - 3 * (k // 2)


def _dispatch_kernel(parts, cap, x_ref, idx_ref, w1_ref, w3_ref, w2_ref, rows_ref, p1_ref, p3_ref, p2_ref,
                     ag0, ag1, ag2, st0, st1, st2, meta, tri, ag_send, ag_recv, mt_send, mt_recv,
                     blk_send, blk_recv, loc_sem, w_send, w_recv):
    me, tp = lax.axis_index("ep"), lax.axis_index("tp")
    m = _coords(me)
    ags, sts = (ag0, ag1, ag2), (st0, st1, st2)
    t_loc = x_ref.shape[0]
    _barrier(m, tp)

    w_copies = [pltpu.make_async_remote_copy(s, d, w_send.at[i], w_recv.at[i], device_id={"tp": 1 - tp},
                                             device_id_type=MESH)
                for i, (s, d) in enumerate(((w1_ref, p1_ref), (w3_ref, p3_ref), (w2_ref, p2_ref)))]

    def source(c, i, own):
        off, w = parts[c]
        return (x_ref.at[:, pl.ds(off, w)], idx_ref) if own else (ags[c].at[i], meta.at[c, i])

    def row_copies(c, i_from, i_to, own, axis, d):
        src, mt = source(c, i_from, own)
        to = {"ep": _shift(m, {axis: d})}
        return (pltpu.make_async_remote_copy(src, ags[c].at[i_to], ag_send.at[c, i_to], ag_recv.at[c, i_to],
                                             device_id=to, device_id_type=MESH),
                pltpu.make_async_remote_copy(mt, meta.at[c, i_to], mt_send.at[c, i_to], mt_recv.at[c, i_to],
                                             device_id=to, device_id_type=MESH))

    def start(copies):
        for cp in reversed(copies):
            cp.start()

    def block_copy(c, i, d3):
        a1, a2, a3 = _color(c)
        off, w = parts[c]
        src = _shift(m, {a1: N_AX - i // 4, a2: N_AX - i % 4})
        part = sts[c].at[i, pl.ds(d3 * cap, cap)]
        dst = rows_ref.at[pl.ds(pl.multiple_of(src * cap, cap), cap), pl.ds(off, w)]
        if d3 == 0:
            return pltpu.make_async_copy(part, dst, loc_sem.at[c, i])
        return pltpu.make_async_remote_copy(part, dst, blk_send.at[c, i, d3 - 1], blk_recv,
                                            device_id={"ep": _shift(m, {a3: d3})}, device_id_type=MESH)

    def process(c, i, own):
        _, _, a3 = _color(c)
        off, w = parts[c]
        ids = idx_ref[...] if own else meta[c, i]
        member = [jnp.max((ids == _shift(m, {a3: d3})).astype(F32), axis=0, keepdims=True) for d3 in range(N_AX)]
        table = jnp.concatenate(member + [jnp.zeros((4, t_loc), F32)], axis=0)
        slots = jnp.dot(table.astype(BF), tri[...], preferred_element_type=F32)
        key = jnp.where(table > 0, slots, -1.0)
        want = lax.broadcasted_iota(jnp.int32, (cap, t_loc), 0).astype(F32)
        pick = jnp.concatenate([jnp.where(key[d3:d3 + 1] == want, 1.0, 0.0) for d3 in range(N_AX)], axis=0)
        xs = x_ref[:, off:off + w] if own else ags[c][i]
        sts[c][i] = jnp.dot(pick.astype(BF), xs, preferred_element_type=F32).astype(BF)
        for d3 in (1, 3, 2, 0):
            block_copy(c, i, d3).start()

    for c in range(AXES):
        a1, a2, _ = _color(c)
        for d in (1, 3, 2):
            start(row_copies(c, 0, d * 4, True, a1, d))
        for d in (1, 3, 2):
            start(row_copies(c, 0, d, True, a2, d))
    for cp in w_copies:
        cp.start()
    r = lax.broadcasted_iota(jnp.int32, (t_loc, t_loc), 0)
    q = lax.broadcasted_iota(jnp.int32, (t_loc, t_loc), 1)
    tri[...] = jnp.where(r < q, 1.0, 0.0).astype(BF)
    for c in range(AXES):
        process(c, 0, True)

    def wait_rows(c, i):
        for cp in row_copies(c, i, i, False, 0, 1):
            cp.wait_recv()

    def relay(k, carry):
        d1 = _order(k)
        for c in range(AXES):
            wait_rows(c, d1 * 4)
            for d in (1, 3, 2):
                start(row_copies(c, d1 * 4, d1 * 4 + d, False, _color(c)[1], d))
        for c in range(AXES):
            process(c, d1 * 4, False)
        return carry

    lax.fori_loop(0, 3, relay, 0)

    def rest(k, carry):
        d2, k1 = _order(k // 4), k % 4
        i = k1 * 4 + d2
        for c in range(AXES):
            wait_rows(c, i)
            process(c, i, False)
        return carry

    lax.fori_loop(0, 12, rest, 0)

    def drain(i, carry):
        for c in range(AXES):
            for d3 in range(1, N_AX):
                block_copy(c, i, d3).wait_send()
            block_copy(c, i, 0).wait()
        return carry

    lax.fori_loop(0, 16, drain, 0)

    def drain_rows(i, carry):
        for c in range(AXES):
            for cp in row_copies(c, i, i, False, 0, 1):
                cp.wait_send()
        return carry

    lax.fori_loop(1, 16, drain_rows, 0)
    for cp in w_copies:
        cp.wait()
    n_in = rows_ref.shape[0] * 3 // 4
    pltpu.make_async_copy(rows_ref.at[pl.ds(0, n_in)], rows_ref.at[pl.ds(0, n_in)], blk_recv).wait()


def _dispatch(x, idx_t, w1, w3, w2, n_exp, cap):
    t_loc, d = x.shape
    parts = ((0, d * 3 // 8), (d * 3 // 8, d * 5 // 16), (d * 11 // 16, d * 5 // 16))
    any_spec = pl.BlockSpec(memory_space=pl.ANY)
    vm = pl.BlockSpec(memory_space=pltpu.VMEM)
    dma = pltpu.SemaphoreType.DMA
    out = [jax.ShapeDtypeStruct((n_exp * cap, d), x.dtype)] + [jax.ShapeDtypeStruct(w.shape, w.dtype) for w in (w1, w3, w2)]
    return pl.pallas_call(
        functools.partial(_dispatch_kernel, parts, cap),
        out_shape=out,
        in_specs=[vm, vm, any_spec, any_spec, any_spec],
        out_specs=[any_spec] * 4,
        scratch_shapes=[pltpu.VMEM((16, t_loc, w), BF) for _, w in parts]
        + [pltpu.VMEM((16, 4 * cap, w), BF) for _, w in parts]
        + [pltpu.VMEM((3, 16) + idx_t.shape, jnp.int32), pltpu.VMEM((t_loc, t_loc), BF),
           dma((3, 16)), dma((3, 16)), dma((3, 16)), dma((3, 16)), dma((3, 16, 3)), dma, dma((3, 16)),
           dma((3,)), dma((3,))],
        compiler_params=pltpu.CompilerParams(collective_id=0, has_side_effects=True, vmem_limit_bytes=VMEM_LIMIT),
        name="dispatch",
    )(x, idx_t, w1, w3, w2)


def _expert_kernel(x_ref, w1a, w3a, w2a, w1b, w3b, w2b, y_ref):
    x = x_ref[...]
    y = None
    for w1, w3, w2 in ((w1a, w3a, w2a), (w1b, w3b, w2b)):
        a = jnp.dot(x, w1[...], preferred_element_type=F32)
        b = jnp.dot(x, w3[...], preferred_element_type=F32)
        h = (jax.nn.silu(a) * b).astype(BF)
        part = jnp.dot(h, w2[...], preferred_element_type=F32)
        y = part if y is None else y + part
    y_ref[...] = y.astype(BF)


def _experts(rows, w1a, w3a, w2a, w1b, w3b, w2b):
    n, d = rows.shape
    f = w1a.shape[1]
    blk = 256
    wide = pl.BlockSpec((d, f), lambda i: (0, 0), pipeline_mode=pl.Buffered(1))
    tall = pl.BlockSpec((f, d), lambda i: (0, 0), pipeline_mode=pl.Buffered(1))
    return pl.pallas_call(
        _expert_kernel,
        out_shape=jax.ShapeDtypeStruct((n, d), BF),
        grid=(n // blk,),
        in_specs=[pl.BlockSpec((blk, d), lambda i: (i, 0)), wide, wide, tall, wide, wide, tall],
        out_specs=pl.BlockSpec((blk, d), lambda i: (i, 0)),
        compiler_params=pltpu.CompilerParams(vmem_limit_bytes=VMEM_LIMIT),
        cost_estimate=pl.CostEstimate(flops=12 * n * d * f, bytes_accessed=4 * n * d + 12 * d * f, transcendentals=2 * n * f),
        name="experts",
    )(rows, w1a, w3a, w2a, w1b, w3b, w2b)


def _split3(v):
    hi = v.astype(BF)
    r = v - hi.astype(F32)
    mid = r.astype(BF)
    return hi, mid, (r - mid.astype(F32)).astype(BF)


def _combine_kernel(cap, idx_ref, g_ref, back_ref, y_ref, key, gates, acc):
    t_loc, top = idx_ref.shape
    n_exp = key.shape[1]
    i = pl.program_id(0)

    @pl.when(i == 0)
    def _():
        e = lax.broadcasted_iota(jnp.int32, (t_loc, n_exp), 1)
        member = jnp.zeros((t_loc, n_exp), F32)
        gate = jnp.zeros((t_loc, n_exp), F32)
        for j in range(top):
            hit = idx_ref[:, j:j + 1] == e
            member = jnp.where(hit, 1.0, member)
            gate = jnp.where(hit, g_ref[:, j:j + 1], gate)
        r = lax.broadcasted_iota(jnp.int32, (t_loc, t_loc), 0)
        q = lax.broadcasted_iota(jnp.int32, (t_loc, t_loc), 1)
        lower = jnp.where(q < r, 1.0, 0.0).astype(BF)
        slots = jnp.dot(lower, member.astype(BF), preferred_element_type=F32)
        key[...] = jnp.where(member > 0, slots, -1.0).astype(BF)
        for k, part in enumerate(_split3(gate)):
            gates[k] = part
        acc[...] = jnp.zeros_like(acc)

    wide = back_ref.shape[0]
    e = lax.broadcasted_iota(jnp.int32, (n_exp, wide), 0)
    col = lax.broadcasted_iota(jnp.int32, (n_exp, wide), 1)
    spread = jnp.where(e == i * (wide // cap) + col // cap, 1.0, 0.0).astype(BF)
    slot = (lax.broadcasted_iota(jnp.int32, (t_loc, wide), 1) % cap).astype(F32)
    hit = jnp.dot(key[...], spread, preferred_element_type=F32) == slot
    total = acc[...]
    for k in range(3):
        weight = jnp.where(hit, jnp.dot(gates[k], spread, preferred_element_type=F32), 0.0).astype(BF)
        total += jnp.dot(weight, back_ref[...], preferred_element_type=F32)
    acc[...] = total

    @pl.when(i == pl.num_programs(0) - 1)
    def _():
        y_ref[...] = acc[...].astype(BF)


def _combine(idx, g, back, n_exp, cap):
    t_loc, top = idx.shape
    d = back.shape[1]
    blk = 256
    return pl.pallas_call(
        functools.partial(_combine_kernel, cap),
        out_shape=jax.ShapeDtypeStruct((t_loc, d), BF),
        grid=(back.shape[0] // blk,),
        in_specs=[pl.BlockSpec((t_loc, top), lambda i: (0, 0)), pl.BlockSpec((t_loc, top), lambda i: (0, 0)),
                  pl.BlockSpec((blk, d), lambda i: (i, 0))],
        out_specs=pl.BlockSpec((t_loc, d), lambda i: (0, 0)),
        scratch_shapes=[pltpu.VMEM((t_loc, n_exp), BF), pltpu.VMEM((3, t_loc, n_exp), BF), pltpu.VMEM((t_loc, d), F32)],
        compiler_params=pltpu.CompilerParams(vmem_limit_bytes=VMEM_LIMIT),
        name="combine",
    )(idx, g, back)


def solution(mesh):
    ep = mesh.shape["ep"]
    rows = P(("dp", "ep", "tp"), None)

    def local(x, idx, g, w1, w3, w2):
        t_loc, d = x.shape
        top = idx.shape[1]
        cap = CF * top * t_loc // ep
        w1, w3, w2 = w1[0], w3[0], w2[0]
        xe, w1b, w3b, w2b = _dispatch(x, idx.T, w1, w3, w2, ep, cap)
        y = _experts(xe, w1, w3, w2, w1b, w3b, w2b)
        back = lax.all_to_all(y.reshape(ep, cap, d), "ep", 0, 0, tiled=True).reshape(ep * cap, d)
        return _combine(idx, g, back, ep, cap)

    return jax.shard_map(local, mesh=mesh,
                         in_specs=(rows, rows, rows, P("ep", None, "tp"), P("ep", None, "tp"), P("ep", "tp", None)),
                         out_specs=rows, check_vma=False)
```

time: 836 us -> 528 us (0.63); the launches traced: 823 us -> 526 us
  blocking collectives: 296 us -> 0 us
  Pallas kernels: 0 us -> 240 us
  matrix products: 70 us -> 0 us
  waiting for transfers between devices: 331 us -> 276 us
  other arithmetic: 53.2 us -> 0 us
  local copies, waits for them, and re-layouts: 49.2 us -> 1.57 us
  between operations: 13.7 us -> 0.03 us
    all_to_all x2 -> x0, blocking collectives: 296 us -> none  [the longest x1 226 us: local(): recv = lax.all_to_all(buf, 'ep', 0, 0, tiled=True)]
    pallas_call x0 -> x3, Pallas kernels: none -> 240 us  [the longest x1 152 us: _dispatch(): pl.pallas_call(functools.partial(_dispatch_kernel, parts, cap), out_shape...]
    dot_general x2 -> x0, matrix products: 70 us -> none  [the longest x1 44.6 us: local(): jnp.einsum('erf,efd->erd', h, w2, preferred_element_type=jnp.float32)]
    all_gather x1 -> x0, waiting for transfers between devices: 57.6 us -> none  [local(): allr = lax.all_gather(recv, 'tp', axis=0)]
    reduce_sum x3 -> x0, other arithmetic: 33.3 us -> none  [the longest x1 20.8 us: local(): y = jnp.sum(parts.astype(jnp.float32), axis=0).astype(jnp.bfloat16)]
    gather x1 -> x0, local copies, waits for them, and re-layouts: 24.4 us -> none  [local(): back[jnp.minimum(dest, n_exp * cap - 1)].astype(jnp.float32)]
    scatter x1 -> x0, local copies, waits for them, and re-layouts: 21.9 us -> none  [local(): jnp.zeros((n_exp * cap, d), x.dtype).at[dest].set(xr, mode='drop')]
    another operation x2 -> x0, other arithmetic: 18.3 us -> none
  transfers between devices with their start and end apart: 2 -> 1, of which waited for: 2 -> 1; matrix products, arithmetic and copies ran while one was open for 0% -> 0% of each run, Pallas kernels for 0% -> 0%
where the time goes in v1:
time: 528 us; the launch traced here: 526 us
  waiting for transfers between devices  276 us (52%)
  Pallas kernels  240 us (45%)
  starting transfers between devices  8.1 us (2%)
    all_to_all x1, waiting for transfers between devices, local(): lax.all_to_all(y.reshape(ep, cap, d), 'ep', 0, 0, tiled=True)  276 us
    pallas_call x1, Pallas kernels, _dispatch(): pl.pallas_call(functools.partial(_dispatch_kernel, parts, cap), out_shape...  152 us
    pallas_call x1, Pallas kernels, _experts(): pl.pallas_call(_expert_kernel, out_shape=jax.ShapeDtypeStruct((n, d), BF)...  62.3 us
    pallas_call x1, Pallas kernels, _combine(): pl.pallas_call(functools.partial(_combine_kernel, cap), out_shape=jax.Sha...  25.9 us
  transfers between devices with their start and end apart: 1, of which 1 were waited for; matrix products, arithmetic and copies ran while one was open for 0% of the time, Pallas kernels for 0%

profile of v1, /device:TPU:0, one launch (start us, length us, event | category | flops | bytes accessed | tf_op | source)
XLA Modules:
  0.0 525.9 jit_solution(6300340835472708131)
XLA Ops:
  0.0 152.0 %dispatch.1 = (bf16[4096,2048]{1,0:T(8,128)(2,1)}, bf16[2048,512]{1,0:T(8,128)(2,1)}, bf16[2048,512]{1,0:T(8,128)(2,1)}, bf16[512,2048]{1,0:T(8,128)(2,1)}) custom-call(bf16[256,2048]{1,0:T(8,128)(2,1)} %x_ref.1, s32[8,256]{1,0:T(8,128)} %bitcast.13, bf16[2048,512]{1,0:T(8,128)(2,1)} %bitcast.7, bf16[2048,512]{1,0:T(8,128)(2,1)} %bitcast.9, ...), custom_call_target="tpu_custom_call" | custom-call | tf_op jit(solution)/shard_map/dispatch/pallas_call | solution.py:168
  152.1 62.3 %experts.1 = bf16[4096,2048]{1,0:T(8,128)(2,1)} custom-call(bf16[4096,2048]{1,0:T(8,128)(2,1)} %get-tuple-element.9.x_ref, bf16[2048,512]{1,0:T(8,128)(2,1)} %bitcast.8, bf16[2048,512]{1,0:T(8,128)(2,1)} %bitcast.10, bf16[512,2048]{1,0:T(8,128)(2,1)} %bitcast.12, bf16[2048,512]{1,0:T(8,128)(2,1)} %get-tuple-element.10.w1b, ...), custom_call_target="tpu_custom_call" | custom-call | flops 51539607552 | bytes 46137344 | tf_op jit(solution)/shard_map/experts/pallas_call | solution.py:201
  214.4 0.0 copy-start
  214.4 0.0 copy-start.1
  214.4 8.1 %all-to-all-start = ((bf16[64,64,2048]{2,1,0:T(8,128)(2,1)}), bf16[64,64,2048]{2,1,0:T(8,128)(2,1)}, u32[]{:S(2)}, u32[]{:S(2)}) async-start(bf16[64,64,2048]{2,1,0:T(8,128)(2,1)} %bitcast.6), calls=%async_computation | async-start | bytes 33554432 | tf_op jit(solution)/shard_map/all_to_all | solution.py:288
  222.5 0.0 copy-done
  222.5 0.8 copy.7.idx_ref
  223.3 0.0 copy-done.1
  223.3 0.8 copy.8.g_ref
  224.1 276.0 %all-to-all-done = bf16[64,64,2048]{2,1,0:T(8,128)(2,1)} async-done(((bf16[64,64,2048]{2,1,0:T(8,128)(2,1)}), bf16[64,64,2048]{2,1,0:T(8,128)(2,1)}, u32[]{:S(2)}, u32[]{:S(2)}) %all-to-all-start) | async-done | bytes 16777248 | tf_op jit(solution)/shard_map/all_to_all | solution.py:288
  500.0 25.9 %combine.1 = bf16[256,2048]{1,0:T(8,128)(2,1)} custom-call(s32[256,8]{1,0:T(8,128)} %copy.7.idx_ref, f32[256,8]{1,0:T(8,128)} %copy.8.g_ref, bf16[4096,2048]{1,0:T(8,128)(2,1)} %bitcast.5.back_ref), custom_call_target="tpu_custom_call" | custom-call | tf_op jit(solution)/shard_map/combine/pallas_call | solution.py:264
Async XLA Ops:
  214.4 8.1 %copy-start = (s32[256,8]{0,1:T(8,128)S(1)}, s32[256,8]{0,1:T(8,128)}, u32[]{:S(2)}) copy-start(s32[256,8]{0,1:T(8,128)} %param.7) | copy-start | bytes 24580
  214.4 8.9 %copy-start.1 = (f32[256,8]{0,1:T(8,128)S(1)}, f32[256,8]{0,1:T(8,128)}, u32[]{:S(2)}) copy-start(f32[256,8]{0,1:T(8,128)} %param.8) | copy-start | bytes 24580
  214.4 285.7 %all-to-all-start = ((bf16[64,64,2048]{2,1,0:T(8,128)(2,1)}), bf16[64,64,2048]{2,1,0:T(8,128)(2,1)}, u32[]{:S(2)}, u32[]{:S(2)}) async-start(bf16[64,64,2048]{2,1,0:T(8,128)(2,1)} %bitcast.6), calls=%async_computation | async-start | bytes 33554432 | tf_op jit(solution)/shard_map/all_to_all | solution.py:288

commit v2 on v1

--- a/solution.py
+++ b/solution.py
@@ -73,7 +73,7 @@
     def block_copy(c, i, d3):
         a1, a2, a3 = _color(c)
         off, w = parts[c]
-        src = _shift(m, {a1: N_AX - i // 4, a2: N_AX - i % 4})
+        src = (i // 4) * N_AX**a1 + (i % 4) * N_AX**a2 + d3 * N_AX**a3
         part = sts[c].at[i, pl.ds(d3 * cap, cap)]
         dst = rows_ref.at[pl.ds(pl.multiple_of(src * cap, cap), cap), pl.ds(off, w)]
         if d3 == 0:
@@ -160,7 +160,7 @@
 
 def _dispatch(x, idx_t, w1, w3, w2, n_exp, cap):
     t_loc, d = x.shape
-    parts = ((0, d * 3 // 8), (d * 3 // 8, d * 5 // 16), (d * 11 // 16, d * 5 // 16))
+    parts = _parts(d)
     any_spec = pl.BlockSpec(memory_space=pl.ANY)
     vm = pl.BlockSpec(memory_space=pltpu.VMEM)
     dma = pltpu.SemaphoreType.DMA
@@ -180,36 +180,6 @@
     )(x, idx_t, w1, w3, w2)
 
 
-def _expert_kernel(x_ref, w1a, w3a, w2a, w1b, w3b, w2b, y_ref):
-    x = x_ref[...]
-    y = None
-    for w1, w3, w2 in ((w1a, w3a, w2a), (w1b, w3b, w2b)):
-        a = jnp.dot(x, w1[...], preferred_element_type=F32)
-        b = jnp.dot(x, w3[...], preferred_element_type=F32)
-        h = (jax.nn.silu(a) * b).astype(BF)
-        part = jnp.dot(h, w2[...], preferred_element_type=F32)
-        y = part if y is None else y + part
-    y_ref[...] = y.astype(BF)
-
-
-def _experts(rows, w1a, w3a, w2a, w1b, w3b, w2b):
-    n, d = rows.shape
-    f = w1a.shape[1]
-    blk = 256
-    wide = pl.BlockSpec((d, f), lambda i: (0, 0), pipeline_mode=pl.Buffered(1))
-    tall = pl.BlockSpec((f, d), lambda i: (0, 0), pipeline_mode=pl.Buffered(1))
-    return pl.pallas_call(
-        _expert_kernel,
-        out_shape=jax.ShapeDtypeStruct((n, d), BF),
-        grid=(n // blk,),
-        in_specs=[pl.BlockSpec((blk, d), lambda i: (i, 0)), wide, wide, tall, wide, wide, tall],
-        out_specs=pl.BlockSpec((blk, d), lambda i: (i, 0)),
-        compiler_params=pltpu.CompilerParams(vmem_limit_bytes=VMEM_LIMIT),
-        cost_estimate=pl.CostEstimate(flops=12 * n * d * f, bytes_accessed=4 * n * d + 12 * d * f, transcendentals=2 * n * f),
-        name="experts",
-    )(rows, w1a, w3a, w2a, w1b, w3b, w2b)
-
-
 def _split3(v):
     hi = v.astype(BF)
     r = v - hi.astype(F32)
@@ -217,61 +187,243 @@
     return hi, mid, (r - mid.astype(F32)).astype(BF)
 
 
-def _combine_kernel(cap, idx_ref, g_ref, back_ref, y_ref, key, gates, acc):
+def _pack(idx_ref, g_ref, n_exp):
     t_loc, top = idx_ref.shape
-    n_exp = key.shape[1]
-    i = pl.program_id(0)
-
-    @pl.when(i == 0)
-    def _():
-        e = lax.broadcasted_iota(jnp.int32, (t_loc, n_exp), 1)
-        member = jnp.zeros((t_loc, n_exp), F32)
-        gate = jnp.zeros((t_loc, n_exp), F32)
-        for j in range(top):
-            hit = idx_ref[:, j:j + 1] == e
-            member = jnp.where(hit, 1.0, member)
-            gate = jnp.where(hit, g_ref[:, j:j + 1], gate)
-        r = lax.broadcasted_iota(jnp.int32, (t_loc, t_loc), 0)
-        q = lax.broadcasted_iota(jnp.int32, (t_loc, t_loc), 1)
-        lower = jnp.where(q < r, 1.0, 0.0).astype(BF)
-        slots = jnp.dot(lower, member.astype(BF), preferred_element_type=F32)
-        key[...] = jnp.where(member > 0, slots, -1.0).astype(BF)
-        for k, part in enumerate(_split3(gate)):
-            gates[k] = part
-        acc[...] = jnp.zeros_like(acc)
-
-    wide = back_ref.shape[0]
-    e = lax.broadcasted_iota(jnp.int32, (n_exp, wide), 0)
-    col = lax.broadcasted_iota(jnp.int32, (n_exp, wide), 1)
-    spread = jnp.where(e == i * (wide // cap) + col // cap, 1.0, 0.0).astype(BF)
-    slot = (lax.broadcasted_iota(jnp.int32, (t_loc, wide), 1) % cap).astype(F32)
-    hit = jnp.dot(key[...], spread, preferred_element_type=F32) == slot
-    total = acc[...]
-    for k in range(3):
-        weight = jnp.where(hit, jnp.dot(gates[k], spread, preferred_element_type=F32), 0.0).astype(BF)
-        total += jnp.dot(weight, back_ref[...], preferred_element_type=F32)
-    acc[...] = total
-
-    @pl.when(i == pl.num_programs(0) - 1)
-    def _():
-        y_ref[...] = acc[...].astype(BF)
-
-
-def _combine(idx, g, back, n_exp, cap):
-    t_loc, top = idx.shape
-    d = back.shape[1]
-    blk = 256
+    e = lax.broadcasted_iota(jnp.int32, (t_loc, n_exp), 1)
+    member = jnp.zeros((t_loc, n_exp), F32)
+    gate = jnp.zeros((t_loc, n_exp), F32)
+    for j in range(top):
+        hit = idx_ref[:, j:j + 1] == e
+        member = jnp.where(hit, 1.0, member)
+        gate = jnp.where(hit, g_ref[:, j:j + 1], gate)
+    r = lax.broadcasted_iota(jnp.int32, (t_loc, t_loc), 0)
+    q = lax.broadcasted_iota(jnp.int32, (t_loc, t_loc), 1)
+    lower = jnp.where(q < r, 1.0, 0.0).astype(BF)
+    slots = jnp.dot(lower, member.astype(BF), preferred_element_type=F32)
+    key = jnp.where(member > 0, slots, -1.0).astype(BF)
+    return jnp.concatenate((key,) + _split3(gate), axis=1)
+
+
+def _far(d):
+    return N_AX - d
+
+
+def _order4(k):
+    return (1 + 2 * k - 3 * (k // 2)) % N_AX
+
+
+def _return_kernel(parts, cap, ring_n, rows_ref, idx_ref, g_ref, w1a, w3a, w2a, w1b, w3b, w2b, y_ref,
+                   ra0, ra1, ra2, rb0, rb1, rb2, cr0, cr1, cr2, packs, mine, *sems):
+    (x_sem, w_sem, a_send, a_recv, b_send, b_recv, c_send, c_recv, p_send, p_recv) = sems
+    me, tp = lax.axis_index("ep"), lax.axis_index("tp")
+    m = _coords(me)
+    ra, rb, cr = (ra0, ra1, ra2), (rb0, rb1, rb2), (cr0, cr1, cr2)
+    d, f = w1a.shape
+    t_loc = idx_ref.shape[0]
+    n_exp = N_AX**AXES
+    blk = N_AX * cap
+    groups = rows_ref.shape[0] // blk
+    _barrier(m, tp)
+    weights = (w1a, w3a, w2a, w1b, w3b, w2b)
+
+    def p_copy(c, d1):
+        return pltpu.make_async_remote_copy(mine, packs.at[c, d1 - 1], p_send.at[c, d1 - 1], p_recv.at[c, d1 - 1],
+                                            device_id={"ep": _shift(m, {_color(c)[0]: d1})}, device_id_type=MESH)
+
+    def a_wait(c, i):
+        three = ra[c].at[i, pl.ds(0, 3 * cap)]
+        pltpu.make_async_copy(three, three, a_recv.at[c, i]).wait()
+
+    def b_copy(c, d1, d2):
+        i = d1 * 4 + d2
+        return pltpu.make_async_remote_copy(ra[c].at[i], rb[c].at[d1, d2 - 1], b_send.at[c, i], b_recv.at[c, i],
+                                            device_id={"ep": _shift(m, {_color(c)[1]: _far(d2)})}, device_id_type=MESH)
+
+    def forward(k, carry):
+        d1, d2 = _order4(k // 4), k % 4
+        for c in range(AXES):
+            a_wait(c, d1 * 4 + d2)
+
+            @pl.when(d2 > 0)
+            def _():
+                b_copy(c, d1, d2).start()
+        return carry
+
+    def compute(wv1a, wv3a, wv2a, wv1b, wv3b, wv2b, xbuf, ring):
+        vmem = (wv1a, wv3a, wv2a, wv1b, wv3b, wv2b)
+        w_copies = [pltpu.make_async_copy(s, v, w_sem.at[i]) for i, (s, v) in enumerate(zip(weights, vmem))]
+
+        def x_copy(k):
+            return pltpu.make_async_copy(rows_ref.at[pl.ds(k * blk, blk)], xbuf.at[k % 2], x_sem.at[k % 2])
+
+        x_copy(0).start()
+        for cp in w_copies:
+            cp.start()
+        mine[...] = _pack(idx_ref, g_ref, n_exp)
+        for c in range(AXES):
+            for d1 in (1, 3, 2):
+                p_copy(c, d1).start()
+        for cp in w_copies:
+            cp.wait()
+
+        def a_each(k, remote, local):
+            dy, dz = k % 4, k // 4
+            for c in range(AXES):
+                a1, a2, a3 = _color(c)
+                off, w = parts[c]
+                for dx in range(N_AX):
+                    at = (dx, dy, dz)
+                    i, d3 = at[a1] * 4 + at[a2], at[a3]
+
+                    def far(c=c, dx=dx, i=i, d3=d3, off=off, w=w, a3=a3):
+                        remote(pltpu.make_async_remote_copy(
+                            ring.at[k % ring_n, pl.ds(dx * cap, cap), pl.ds(off, w)],
+                            ra[c].at[i, pl.ds(d3 * cap, cap)], a_send.at[k % ring_n, c * 4 + dx], a_recv.at[c, i],
+                            device_id={"ep": _shift(m, {a3: _far(d3)})}, device_id_type=MESH))
+
+                    if c == 0:
+                        far() if dx else local(c, dx, i)
+                    else:
+                        pl.when(d3 > 0)(far)
+                        pl.when(d3 == 0)(lambda c=c, dx=dx, i=i: local(c, dx, i))
+
+        def step(k, carry):
+            x_copy(k).wait()
+
+            @pl.when(k + 1 < groups)
+            def _():
+                x_copy(k + 1).start()
+
+            @pl.when(k >= ring_n)
+            def _():
+                a_each(k - ring_n, lambda cp: cp.wait_send(), lambda c, dx, i: None)
+
+            x = xbuf[k % 2]
+            y = None
+            for w1, w3, w2 in ((wv1a, wv3a, wv2a), (wv1b, wv3b, wv2b)):
+                a = jnp.dot(x, w1[...], preferred_element_type=F32)
+                b = jnp.dot(x, w3[...], preferred_element_type=F32)
+                h = (jax.nn.silu(a) * b).astype(BF)
+                part = jnp.dot(h, w2[...], preferred_element_type=F32)
+                y = part if y is None else y + part
+            ring[k % ring_n] = y.astype(BF)
+
+            def keep(c, dx, i):
+                off, w = parts[c]
+                ra[c][i, 0:cap, :] = ring[k % ring_n, dx * cap:(dx + 1) * cap, off:off + w]
+
+            a_each(k, lambda cp: cp.start(), keep)
+            return carry
+
+        lax.fori_loop(0, groups, step, 0)
+        lax.fori_loop(0, groups, forward, 0)
+
+        def drain(k, carry):
+            a_each(k, lambda cp: cp.wait_send(), lambda c, dx, i: None)
+            return carry
+
+        lax.fori_loop(groups - ring_n, groups, drain, 0)
+
+    pl.run_scoped(compute, *[pltpu.VMEM(w.shape, BF) for w in weights], pltpu.VMEM((2, blk, d), BF),
+                  pltpu.VMEM((ring_n, blk, d), BF))
+
+    def combine(acc, cs0, cs1, cs2):
+        cs = (cs0, cs1, cs2)
+
+        def partial_sum(c, d1, own):
+            _, a2, a3 = _color(c)
+            off, w = parts[c]
+            table = mine[...] if own else packs[c, d1 - 1]
+            row = lax.broadcasted_iota(jnp.int32, (N_AX * n_exp, blk), 0)
+            col = lax.broadcasted_iota(jnp.int32, (N_AX * n_exp, blk), 1)
+            slot = (lax.broadcasted_iota(jnp.int32, (t_loc, blk), 1) % cap).astype(F32)
+            total = None
+            for d2 in range(N_AX):
+                base = _shift(m, {a2: d2}) - m[a3] * N_AX**a3
+                e = base + ((m[a3] + col // cap) % N_AX) * N_AX**a3
+                spread = [jnp.where(row == e + n_exp * k, 1.0, 0.0).astype(BF) for k in range(4)]
+                hit = jnp.dot(table, spread[0], preferred_element_type=F32) == slot
+                data = ra[c][d1 * 4] if d2 == 0 else rb[c][d1, d2 - 1]
+                for k in range(1, 4):
+                    gate = jnp.dot(table, spread[k], preferred_element_type=F32)
+                    part = jnp.dot(jnp.where(hit, gate, 0.0).astype(BF), data, preferred_element_type=F32)
+                    total = part if total is None else total + part
+            return total
+
+        def b_wait(c, d1):
+            for d2 in range(1, N_AX):
+                b_copy(c, d1, d2).wait_recv()
+
+        def c_copy(c, d1):
+            return pltpu.make_async_remote_copy(cs[c].at[d1 - 1], cr[c].at[d1 - 1], c_send.at[c, d1 - 1],
+                                                c_recv.at[c, d1 - 1],
+                                                device_id={"ep": _shift(m, {_color(c)[0]: _far(d1)})},
+                                                device_id_type=MESH)
+
+        for c in range(AXES):
+            for d1 in range(1, N_AX):
+                p_copy(c, d1).wait_recv()
+
+        def send(k, carry):
+            d1 = _order(k)
+            for c in range(AXES):
+                b_wait(c, d1)
+                cs[c][d1 - 1] = partial_sum(c, d1, False)
+                c_copy(c, d1).start()
+            return carry
+
+        lax.fori_loop(0, N_AX - 1, send, 0)
+        for c in range(AXES):
+            off, w = parts[c]
+            b_wait(c, 0)
+            acc[:, off:off + w] = partial_sum(c, 0, True)
+        for c in range(AXES):
+            off, w = parts[c]
+            for d1 in range(1, N_AX):
+                c_copy(c, d1).wait()
+            y_ref[:, off:off + w] = (acc[:, off:off + w] + cr[c][0] + cr[c][1] + cr[c][2]).astype(BF)
+
+    pl.run_scoped(combine, pltpu.VMEM((t_loc, d), F32), *[pltpu.VMEM((3, t_loc, w), F32) for _, w in parts])
+
+    def drain_b(k, carry):
+        for c in range(AXES):
+            for d2 in range(1, N_AX):
+                b_copy(c, k, d2).wait_send()
+        return carry
+
+    lax.fori_loop(0, N_AX, drain_b, 0)
+    for c in range(AXES):
+        for d1 in range(1, N_AX):
+            p_copy(c, d1).wait_send()
+
+
+def _parts(d):
+    return (0, d * 3 // 8), (d * 3 // 8, d * 5 // 16), (d * 11 // 16, d * 5 // 16)
+
+
+def _return(rows, idx, g, weights, cap):
+    n, d = rows.shape
+    t_loc = idx.shape[0]
+    parts = _parts(d)
+    blk = N_AX * cap
+    ring_n = 6
+    any_spec = pl.BlockSpec(memory_space=pl.ANY)
+    vm = pl.BlockSpec(memory_space=pltpu.VMEM)
+    dma = pltpu.SemaphoreType.DMA
     return pl.pallas_call(
-        functools.partial(_combine_kernel, cap),
+        functools.partial(_return_kernel, parts, cap, ring_n),
         out_shape=jax.ShapeDtypeStruct((t_loc, d), BF),
-        grid=(back.shape[0] // blk,),
-        in_specs=[pl.BlockSpec((t_loc, top), lambda i: (0, 0)), pl.BlockSpec((t_loc, top), lambda i: (0, 0)),
-                  pl.BlockSpec((blk, d), lambda i: (i, 0))],
-        out_specs=pl.BlockSpec((t_loc, d), lambda i: (0, 0)),
-        scratch_shapes=[pltpu.VMEM((t_loc, n_exp), BF), pltpu.VMEM((3, t_loc, n_exp), BF), pltpu.VMEM((t_loc, d), F32)],
-        compiler_params=pltpu.CompilerParams(vmem_limit_bytes=VMEM_LIMIT),
-        name="combine",
-    )(idx, g, back)
+        in_specs=[any_spec, vm, vm] + [any_spec] * 6,
+        out_specs=vm,
+        scratch_shapes=[pltpu.VMEM((16, blk, w), BF) for _, w in parts]
+        + [pltpu.VMEM((N_AX, 3, blk, w), BF) for _, w in parts]
+        + [pltpu.VMEM((3, t_loc, w), F32) for _, w in parts]
+        + [pltpu.VMEM((3, 3, t_loc, 4 * N_AX**AXES), BF), pltpu.VMEM((t_loc, 4 * N_AX**AXES), BF),
+           dma((2,)), dma((6,)), dma((ring_n, 12)), dma((3, 16)), dma((3, 16)), dma((3, 16)), dma((3, 3)), dma((3, 3)),
+           dma((3, 3)), dma((3, 3))],
+        compiler_params=pltpu.CompilerParams(collective_id=1, has_side_effects=True, vmem_limit_bytes=63 * 2**20),
+        name="experts_return",
+    )(rows, idx, g, *weights)
 
 
 def solution(mesh):
@@ -284,9 +436,7 @@
         cap = CF * top * t_loc // ep
         w1, w3, w2 = w1[0], w3[0], w2[0]
         xe, w1b, w3b, w2b = _dispatch(x, idx.T, w1, w3, w2, ep, cap)
-        y = _experts(xe, w1, w3, w2, w1b, w3b, w2b)
-        back = lax.all_to_all(y.reshape(ep, cap, d), "ep", 0, 0, tiled=True).reshape(ep * cap, d)
-        return _combine(idx, g, back, ep, cap)
+        return _return(xe, idx, g, (w1, w3, w2, w1b, w3b, w2b), cap)
 
     return jax.shard_map(local, mesh=mesh,
                          in_specs=(rows, rows, rows, P("ep", None, "tp"), P("ep", None, "tp"), P("ep", "tp", None)),

time: 528 us -> 357 us (0.68)
  waiting for transfers between devices: 276 us -> 0 us
  Pallas kernels: 240 us -> 351 us
  starting transfers between devices: 8.1 us -> 0 us
    all_to_all x1 -> x0, waiting for transfers between devices: 276 us -> none  [local(): lax.all_to_all(y.reshape(ep, cap, d), 'ep', 0, 0, tiled=True)]
    pallas_call x2 -> x1, Pallas kernels: 88.2 us -> 199 us  [_return(): pl.pallas_call(functools.partial(_return_kernel, parts, cap, ring_n), out...]
    all_to_all x1 -> x0, starting transfers between devices: 8.1 us -> none  [local(): lax.all_to_all(y.reshape(ep, cap, d), 'ep', 0, 0, tiled=True)]
  transfers between devices with their start and end apart: 1 -> 0, of which waited for: 1 -> 0; matrix products, arithmetic and copies ran while one was open for 0% -> 0% of each run, Pallas kernels for 0% -> 0%
where the time goes in v2:
time: 357 us; the launch traced here: 356 us
  Pallas kernels  351 us (98%)
  local copies, waits for them, and re-layouts  5.28 us (1%)
    pallas_call x1, Pallas kernels, _return(): pl.pallas_call(functools.partial(_return_kernel, parts, cap, ring_n), out...  199 us
    pallas_call x1, Pallas kernels, _dispatch(): pl.pallas_call(functools.partial(_dispatch_kernel, parts, cap), out_shape...  152 us

profile of v2, /device:TPU:0, one launch (start us, length us, event | category | flops | bytes accessed | tf_op | source)
XLA Modules:
  0.0 356.4 jit_solution(16484853605523224248)
XLA Ops:
  0.0 1.5 copy.8.g_ref
  1.5 1.5 copy.7.idx_ref
  3.0 152.0 %dispatch.1 = (bf16[4096,2048]{1,0:T(8,128)(2,1)}, bf16[2048,512]{1,0:T(8,128)(2,1)}, bf16[2048,512]{1,0:T(8,128)(2,1)}, bf16[512,2048]{1,0:T(8,128)(2,1)}) custom-call(bf16[256,2048]{1,0:T(8,128)(2,1)} %x_ref.1, s32[8,256]{1,0:T(8,128)} %bitcast.10, bf16[2048,512]{1,0:T(8,128)(2,1)} %bitcast.4, bf16[2048,512]{1,0:T(8,128)(2,1)} %bitcast.6, ...), custom_call_target="tpu_custom_call" | custom-call | tf_op jit(solution)/shard_map/dispatch/pallas_call | solution.py:168
  155.0 199.0 %experts_return.1 = bf16[256,2048]{1,0:T(8,128)(2,1)} custom-call(bf16[4096,2048]{1,0:T(8,128)(2,1)} %get-tuple-element.9.rows_ref, s32[256,8]{1,0:T(8,128)} %copy.7.idx_ref, f32[256,8]{1,0:T(8,128)} %copy.8.g_ref, bf16[2048,512]{1,0:T(8,128)(2,1)} %bitcast.5, bf16[2048,512]{1,0:T(8,128)(2,1)} %bitcast.7, bf16[512,2048]{1,0:T(8,128)(2,1)} %bitcast.9, ...), custom_call_target="tpu_custom_call" | custom-call | tf_op jit(solution)/shard_map/experts_return/pallas_call | solution.py:413
  354.1 2.3 copy.10

commit v3 on v2

--- a/solution.py
+++ b/solution.py
@@ -28,13 +28,20 @@
     return (c + 1) % 3, (c + 2) % 3, c
 
 
-def _barrier(m, tp):
+def _greet(m, tp):
     bar = pltpu.get_barrier_semaphore()
     for a in range(AXES):
         for d in range(1, N_AX):
             pl.semaphore_signal(bar, inc=1, device_id={"ep": _shift(m, {a: d})}, device_id_type=MESH)
     pl.semaphore_signal(bar, inc=1, device_id={"tp": 1 - tp}, device_id_type=MESH)
-    pl.semaphore_wait(bar, AXES * (N_AX - 1) + 1)
+
+
+def _meet():
+    pl.semaphore_wait(pltpu.get_barrier_semaphore(), AXES * (N_AX - 1) + 1)
+
+
+def _line(k):
+    return k + k // 2 - 2 * (k // 3)
 
 
 def _order(k):
@@ -42,33 +49,45 @@
 
 
 def _dispatch_kernel(parts, cap, x_ref, idx_ref, w1_ref, w3_ref, w2_ref, rows_ref, p1_ref, p3_ref, p2_ref,
-                     ag0, ag1, ag2, st0, st1, st2, meta, tri, ag_send, ag_recv, mt_send, mt_recv,
+                     ag0, ag1, ag2, st0, st1, st2, meta, tri, ag_send, ag_send2, ag_recv, mt_send, mt_recv,
                      blk_send, blk_recv, loc_sem, w_send, w_recv):
     me, tp = lax.axis_index("ep"), lax.axis_index("tp")
     m = _coords(me)
     ags, sts = (ag0, ag1, ag2), (st0, st1, st2)
     t_loc = x_ref.shape[0]
-    _barrier(m, tp)
+    half = t_loc // 2
+    _greet(m, tp)
 
     w_copies = [pltpu.make_async_remote_copy(s, d, w_send.at[i], w_recv.at[i], device_id={"tp": 1 - tp},
                                              device_id_type=MESH)
                 for i, (s, d) in enumerate(((w1_ref, p1_ref), (w3_ref, p3_ref), (w2_ref, p2_ref)))]
 
-    def source(c, i, own):
+    def remote(src, dst, send, recv, axis, d):
+        return pltpu.make_async_remote_copy(src, dst, send, recv, device_id={"ep": _shift(m, {axis: d})},
+                                            device_id_type=MESH)
+
+    def whole(c, i_from, i_to, own, axis, d):
         off, w = parts[c]
-        return (x_ref.at[:, pl.ds(off, w)], idx_ref) if own else (ags[c].at[i], meta.at[c, i])
-
-    def row_copies(c, i_from, i_to, own, axis, d):
-        src, mt = source(c, i_from, own)
-        to = {"ep": _shift(m, {axis: d})}
-        return (pltpu.make_async_remote_copy(src, ags[c].at[i_to], ag_send.at[c, i_to], ag_recv.at[c, i_to],
-                                             device_id=to, device_id_type=MESH),
-                pltpu.make_async_remote_copy(mt, meta.at[c, i_to], mt_send.at[c, i_to], mt_recv.at[c, i_to],
-                                             device_id=to, device_id_type=MESH))
-
-    def start(copies):
-        for cp in reversed(copies):
-            cp.start()
+        src = x_ref.at[:, pl.ds(off, w)] if own else ags[c].at[i_from]
+        return remote(src, ags[c].at[i_to], ag_send.at[c, i_to], ag_recv.at[c, i_to], axis, d)
+
+    def top(c, i_from, i_to, axis):
+        rows = pl.ds(0, half)
+        return remote(ags[c].at[i_from, rows], ags[c].at[i_to, rows], ag_send.at[c, i_to], ag_recv.at[c, i_to], axis, 1)
+
+    def bottom(c, i_from, i_to, axis):
+        rows = pl.ds(half, half)
+        return remote(ags[c].at[i_from, rows], ags[c].at[i_to, rows], ag_send2.at[c, i_to], ag_recv.at[c, i_to], axis, 3)
+
+    def ids_copy(c, i_from, i_to, own, axis, d):
+        src = idx_ref if own else meta.at[c, i_from]
+        return remote(src, meta.at[c, i_to], mt_send.at[c, i_to], mt_recv.at[c, i_to], axis, d)
+
+    def spread(c, i, step, own, axis):
+        for d in (1, 3, 2):
+            ids_copy(c, i, i + d * step, own, axis, d).start()
+        for d in (1, 3):
+            whole(c, i, i + d * step, own, axis, d).start()
 
     def block_copy(c, i, d3):
         a1, a2, a3 = _color(c)
@@ -81,7 +100,7 @@
         return pltpu.make_async_remote_copy(part, dst, blk_send.at[c, i, d3 - 1], blk_recv,
                                             device_id={"ep": _shift(m, {a3: d3})}, device_id_type=MESH)
 
-    def process(c, i, own):
+    def pick(c, i, own):
         _, _, a3 = _color(c)
         off, w = parts[c]
         ids = idx_ref[...] if own else meta[c, i]
@@ -90,51 +109,75 @@
         slots = jnp.dot(table.astype(BF), tri[...], preferred_element_type=F32)
         key = jnp.where(table > 0, slots, -1.0)
         want = lax.broadcasted_iota(jnp.int32, (cap, t_loc), 0).astype(F32)
-        pick = jnp.concatenate([jnp.where(key[d3:d3 + 1] == want, 1.0, 0.0) for d3 in range(N_AX)], axis=0)
+        one_hot = jnp.concatenate([jnp.where(key[d3:d3 + 1] == want, 1.0, 0.0) for d3 in range(N_AX)], axis=0)
         xs = x_ref[:, off:off + w] if own else ags[c][i]
-        sts[c][i] = jnp.dot(pick.astype(BF), xs, preferred_element_type=F32).astype(BF)
+        sts[c][i] = jnp.dot(one_hot.astype(BF), xs, preferred_element_type=F32).astype(BF)
+
+    def send_blocks(c, i):
         for d3 in (1, 3, 2, 0):
             block_copy(c, i, d3).start()
 
-    for c in range(AXES):
-        a1, a2, _ = _color(c)
-        for d in (1, 3, 2):
-            start(row_copies(c, 0, d * 4, True, a1, d))
-        for d in (1, 3, 2):
-            start(row_copies(c, 0, d, True, a2, d))
-    for cp in w_copies:
-        cp.start()
+    def process(i):
+        for c in range(AXES):
+            pick(c, i, False)
+            send_blocks(c, i)
+
+    def wait_rows(c, i):
+        ids_copy(c, i, i, False, 0, 1).wait_recv()
+        whole(c, i, i, False, 0, 1).wait_recv()
+
     r = lax.broadcasted_iota(jnp.int32, (t_loc, t_loc), 0)
     q = lax.broadcasted_iota(jnp.int32, (t_loc, t_loc), 1)
     tri[...] = jnp.where(r < q, 1.0, 0.0).astype(BF)
+    _meet()
     for c in range(AXES):
-        process(c, 0, True)
-
-    def wait_rows(c, i):
-        for cp in row_copies(c, i, i, False, 0, 1):
-            cp.wait_recv()
-
-    def relay(k, carry):
-        d1 = _order(k)
-        for c in range(AXES):
+        a1, a2, _ = _color(c)
+        spread(c, 0, 4, True, a1)
+        spread(c, 0, 1, True, a2)
+    for cp in w_copies:
+        cp.start()
+    for c in range(AXES):
+        pick(c, 0, True)
+        send_blocks(c, 0)
+
+    def pass_on(c, d, i, i_to, axis):
+        pl.when(d == 1)(lambda: top(c, i, i_to, axis).start())
+        pl.when(d == 3)(lambda: bottom(c, i, i_to, axis).start())
+
+    def first_near(k, carry):
+        d1 = 1 + 2 * k
+        for c in range(AXES):
+            a1, a2, _ = _color(c)
             wait_rows(c, d1 * 4)
-            for d in (1, 3, 2):
-                start(row_copies(c, d1 * 4, d1 * 4 + d, False, _color(c)[1], d))
-        for c in range(AXES):
-            process(c, d1 * 4, False)
-        return carry
-
-    lax.fori_loop(0, 3, relay, 0)
-
-    def rest(k, carry):
-        d2, k1 = _order(k // 4), k % 4
-        i = k1 * 4 + d2
-        for c in range(AXES):
-            wait_rows(c, i)
-            process(c, i, False)
-        return carry
-
-    lax.fori_loop(0, 12, rest, 0)
+            pass_on(c, d1, d1 * 4, 8, a1)
+            spread(c, d1 * 4, 1, False, a2)
+        process(d1 * 4)
+        return carry
+
+    def second_near(k, carry):
+        j, d2 = k // 2, 1 + 2 * (k % 2)
+        d1 = _line(j)
+        for c in range(AXES):
+            wait_rows(c, d1 * 4 + d2)
+            pass_on(c, d2, d1 * 4 + d2, d1 * 4 + 2, _color(c)[1])
+        process(d1 * 4 + d2)
+        return carry
+
+    def second_far(k, carry):
+        d1 = _line(k)
+        for c in range(AXES):
+            wait_rows(c, d1 * 4 + 2)
+        process(d1 * 4 + 2)
+        return carry
+
+    lax.fori_loop(0, 2, first_near, 0)
+    lax.fori_loop(0, 2, second_near, 0)
+    for c in range(AXES):
+        wait_rows(c, 8)
+        spread(c, 8, 1, False, _color(c)[1])
+    process(8)
+    lax.fori_loop(2, 8, second_near, 0)
+    lax.fori_loop(0, 4, second_far, 0)
 
     def drain(i, carry):
         for c in range(AXES):
@@ -145,13 +188,26 @@
 
     lax.fori_loop(0, 16, drain, 0)
 
-    def drain_rows(i, carry):
-        for c in range(AXES):
-            for cp in row_copies(c, i, i, False, 0, 1):
-                cp.wait_send()
-        return carry
-
-    lax.fori_loop(1, 16, drain_rows, 0)
+    def drain_far(c, i):
+        top(c, i, i, 0).wait_send()
+        bottom(c, i, i, 0).wait_send()
+
+    def drain_line(d1, carry):
+        for c in range(AXES):
+            for d2 in range(1, N_AX):
+                ids_copy(c, 0, d1 * 4 + d2, False, 0, 1).wait_send()
+            for d2 in (1, 3):
+                whole(c, 0, d1 * 4 + d2, False, 0, 1).wait_send()
+            drain_far(c, d1 * 4 + 2)
+        return carry
+
+    lax.fori_loop(0, N_AX, drain_line, 0)
+    for c in range(AXES):
+        for d1 in range(1, N_AX):
+            ids_copy(c, 0, d1 * 4, False, 0, 1).wait_send()
+        for d1 in (1, 3):
+            whole(c, 0, d1 * 4, False, 0, 1).wait_send()
+        drain_far(c, 8)
     for cp in w_copies:
         cp.wait()
     n_in = rows_ref.shape[0] * 3 // 4
@@ -173,7 +229,7 @@
         scratch_shapes=[pltpu.VMEM((16, t_loc, w), BF) for _, w in parts]
         + [pltpu.VMEM((16, 4 * cap, w), BF) for _, w in parts]
         + [pltpu.VMEM((3, 16) + idx_t.shape, jnp.int32), pltpu.VMEM((t_loc, t_loc), BF),
-           dma((3, 16)), dma((3, 16)), dma((3, 16)), dma((3, 16)), dma((3, 16, 3)), dma, dma((3, 16)),
+           dma((3, 16)), dma((3, 16)), dma((3, 16)), dma((3, 16)), dma((3, 16)), dma((3, 16, 3)), dma, dma((3, 16)),
            dma((3,)), dma((3,))],
         compiler_params=pltpu.CompilerParams(collective_id=0, has_side_effects=True, vmem_limit_bytes=VMEM_LIMIT),
         name="dispatch",
@@ -188,14 +244,15 @@
 
 
 def _pack(idx_ref, g_ref, n_exp):
-    t_loc, top = idx_ref.shape
+    top, t_loc = idx_ref.shape
+    idx, g = idx_ref[...].T, g_ref[...].T
     e = lax.broadcasted_iota(jnp.int32, (t_loc, n_exp), 1)
     member = jnp.zeros((t_loc, n_exp), F32)
     gate = jnp.zeros((t_loc, n_exp), F32)
     for j in range(top):
-        hit = idx_ref[:, j:j + 1] == e
+        hit = idx[:, j:j + 1] == e
         member = jnp.where(hit, 1.0, member)
-        gate = jnp.where(hit, g_ref[:, j:j + 1], gate)
+        gate = jnp.where(hit, g[:, j:j + 1], gate)
     r = lax.broadcasted_iota(jnp.int32, (t_loc, t_loc), 0)
     q = lax.broadcasted_iota(jnp.int32, (t_loc, t_loc), 1)
     lower = jnp.where(q < r, 1.0, 0.0).astype(BF)
@@ -219,11 +276,11 @@
     m = _coords(me)
     ra, rb, cr = (ra0, ra1, ra2), (rb0, rb1, rb2), (cr0, cr1, cr2)
     d, f = w1a.shape
-    t_loc = idx_ref.shape[0]
+    t_loc = idx_ref.shape[1]
     n_exp = N_AX**AXES
     blk = N_AX * cap
     groups = rows_ref.shape[0] // blk
-    _barrier(m, tp)
+    _greet(m, tp)
     weights = (w1a, w3a, w2a, w1b, w3b, w2b)
 
     def p_copy(c, d1):
@@ -260,6 +317,7 @@
         for cp in w_copies:
             cp.start()
         mine[...] = _pack(idx_ref, g_ref, n_exp)
+        _meet()
         for c in range(AXES):
             for d1 in (1, 3, 2):
                 p_copy(c, d1).start()
@@ -403,7 +461,7 @@
 
 def _return(rows, idx, g, weights, cap):
     n, d = rows.shape
-    t_loc = idx.shape[0]
+    t_loc = idx.shape[1]
     parts = _parts(d)
     blk = N_AX * cap
     ring_n = 6
@@ -436,7 +494,7 @@
         cap = CF * top * t_loc // ep
         w1, w3, w2 = w1[0], w3[0], w2[0]
         xe, w1b, w3b, w2b = _dispatch(x, idx.T, w1, w3, w2, ep, cap)
-        return _return(xe, idx, g, (w1, w3, w2, w1b, w3b, w2b), cap)
+        return _return(xe, idx.T, g.T, (w1, w3, w2, w1b, w3b, w2b), cap)
 
     return jax.shard_map(local, mesh=mesh,
                          in_specs=(rows, rows, rows, P("ep", None, "tp"), P("ep", None, "tp"), P("ep", "tp", None)),

time: 357 us -> 334 us (0.936)
  Pallas kernels: 351 us -> 332 us
    pallas_call x1, Pallas kernels: 152 us -> 135 us  [_dispatch(): pl.pallas_call(functools.partial(_dispatch_kernel, parts, cap), out_shape...]
where the time goes in v3:
time: 334 us
  Pallas kernels  332 us (99%)
    pallas_call x1, Pallas kernels, _return(): pl.pallas_call(functools.partial(_return_kernel, parts, cap, ring_n), out...  197 us
    pallas_call x1, Pallas kernels, _dispatch(): pl.pallas_call(functools.partial(_dispatch_kernel, parts, cap), out_shape...  135 us

profile of v3, /device:TPU:0, one launch (start us, length us, event | category | flops | bytes accessed | tf_op | source)
XLA Modules:
  0.0 334.1 jit_solution(15957850096479092007)
XLA Ops:
  0.0 134.8 %dispatch.1 = (bf16[4096,2048]{1,0:T(8,128)(2,1)}, bf16[2048,512]{1,0:T(8,128)(2,1)}, bf16[2048,512]{1,0:T(8,128)(2,1)}, bf16[512,2048]{1,0:T(8,128)(2,1)}) custom-call(bf16[256,2048]{1,0:T(8,128)(2,1)} %x_ref.1, s32[8,256]{1,0:T(8,128)} %bitcast.11, bf16[2048,512]{1,0:T(8,128)(2,1)} %bitcast.5, bf16[2048,512]{1,0:T(8,128)(2,1)} %bitcast.7, ...), custom_call_target="tpu_custom_call" | custom-call | tf_op jit(solution)/shard_map/dispatch/pallas_call | solution.py:224
  134.8 197.0 %experts_return.1 = bf16[256,2048]{1,0:T(8,128)(2,1)} custom-call(bf16[4096,2048]{1,0:T(8,128)(2,1)} %get-tuple-element.9.rows_ref, s32[8,256]{1,0:T(8,128)} %bitcast.12, f32[8,256]{1,0:T(8,128)} %bitcast.13, bf16[2048,512]{1,0:T(8,128)(2,1)} %bitcast.6, bf16[2048,512]{1,0:T(8,128)(2,1)} %bitcast.8, bf16[512,2048]{1,0:T(8,128)(2,1)} %bitcast.10, ...), custom_call_target="tpu_custom_call" | custom-call | tf_op jit(solution)/shard_map/experts_return/pallas_call | solution.py:471
  331.8 2.3 copy.8

commit v4 on v0

v4 whole, which is shorter than its diff:
```python
import functools

import jax
import jax.numpy as jnp
from jax import lax
from jax.experimental import pallas as pl
from jax.experimental.pallas import tpu as pltpu
from jax.sharding import PartitionSpec as P

CF = 2
N_AX = 4
AXES = 3
VMEM_LIMIT = 60 * 2**20
MESH = pl.DeviceIdType.MESH
BF = jnp.bfloat16
F32 = jnp.float32


def _coords(me):
    return [(me // N_AX**a) % N_AX for a in range(AXES)]


def _shift(m, moves):
    return sum(((m[a] + moves.get(a, 0)) % N_AX) * N_AX**a for a in range(AXES))


def _color(c):
    return (c + 1) % 3, (c + 2) % 3, c


def _greet(m, tp):
    bar = pltpu.get_barrier_semaphore()
    for a in range(AXES):
        for d in range(1, N_AX):
            pl.semaphore_signal(bar, inc=1, device_id={"ep": _shift(m, {a: d})}, device_id_type=MESH)
    pl.semaphore_signal(bar, inc=1, device_id={"tp": 1 - tp}, device_id_type=MESH)


def _meet():
    pl.semaphore_wait(pltpu.get_barrier_semaphore(), AXES * (N_AX - 1) + 1)


def _line(k):
    return k + k // 2 - 2 * (k // 3)


def _order(k):
    return 1 + 2 * k - 3 * (k // 2)


def _split3(v):
    hi = v.astype(BF)
    r = v - hi.astype(F32)
    mid = r.astype(BF)
    return hi, mid, (r - mid.astype(F32)).astype(BF)


def _pack(idx_ref, g_ref, n_exp):
    top, t_loc = idx_ref.shape
    idx, g = idx_ref[...].T, g_ref[...].T
    e = lax.broadcasted_iota(jnp.int32, (t_loc, n_exp), 1)
    member = jnp.zeros((t_loc, n_exp), F32)
    gate = jnp.zeros((t_loc, n_exp), F32)
    for j in range(top):
        hit = idx[:, j:j + 1] == e
        member = jnp.where(hit, 1.0, member)
        gate = jnp.where(hit, g[:, j:j + 1], gate)
    r = lax.broadcasted_iota(jnp.int32, (t_loc, t_loc), 0)
    q = lax.broadcasted_iota(jnp.int32, (t_loc, t_loc), 1)
    lower = jnp.where(q < r, 1.0, 0.0).astype(BF)
    slots = jnp.dot(lower, member.astype(BF), preferred_element_type=F32)
    key = jnp.where(member > 0, slots, -1.0).astype(BF)
    return jnp.concatenate((key,) + _split3(gate), axis=1)


def _far(d):
    return N_AX - d


def _order4(k):
    return (1 + 2 * k - 3 * (k // 2)) % N_AX


def _parts(d):
    return (0, d * 3 // 8), (d * 3 // 8, d * 5 // 16), (d * 11 // 16, d * 5 // 16)


def _layer_kernel(parts, cap, ring_n, st_n, x_ref, idx_ref, g_ref, w1_ref, w3_ref, w2_ref, y_ref, rows_ref, cr0, cr1, cr2,
                  ag0, ag1, ag2, ra0, ra1, ra2, wp1, wp3, wp2, meta, packs, mine, tri, *sems):
    (ag_send, ag_send2, ag_recv, mt_send, mt_recv, blk_send, blk_recv, loc_sem, w_send, w_recv, w_loc, x_sem, a_send, a_recv,
     b_send, b_recv, c_send, c_recv, cr_sem, p_send, p_recv, free_sem) = sems
    me, tp = lax.axis_index("ep"), lax.axis_index("tp")
    m = _coords(me)
    ags, ra, cr = (ag0, ag1, ag2), (ra0, ra1, ra2), (cr0, cr1, cr2)
    t_loc, d = x_ref.shape
    n_exp = N_AX**AXES
    half = t_loc // 2
    blk = N_AX * cap
    groups = rows_ref.shape[0] // blk
    _greet(m, tp)

    def remote(src, dst, send, recv, axis, dist):
        return pltpu.make_async_remote_copy(src, dst, send, recv, device_id={"ep": _shift(m, {axis: dist})},
                                            device_id_type=MESH)

    w_refs, w_parts = (w1_ref, w3_ref, w2_ref), (wp1, wp3, wp2)
    w_swaps = [pltpu.make_async_remote_copy(w_refs[i], w_parts[i], w_send.at[i], w_recv.at[i], device_id={"tp": 1 - tp},
                                            device_id_type=MESH) for i in range(3)]


    def whole(c, i_from, i_to, own, axis, dist):
        off, w = parts[c]
        src = x_ref.at[:, pl.ds(off, w)] if own else ags[c].at[i_from]
        return remote(src, ags[c].at[i_to], ag_send.at[c, i_to], ag_recv.at[c, i_to], axis, dist)

    def top(c, i_from, i_to, axis):
        rows = pl.ds(0, half)
        return remote(ags[c].at[i_from, rows], ags[c].at[i_to, rows], ag_send.at[c, i_to], ag_recv.at[c, i_to], axis, 1)

    def bottom(c, i_from, i_to, axis):
        rows = pl.ds(half, half)
        return remote(ags[c].at[i_from, rows], ags[c].at[i_to, rows], ag_send2.at[c, i_to], ag_recv.at[c, i_to], axis, 3)

    def ids_copy(c, i_from, i_to, own, axis, dist):
        src = idx_ref if own else meta.at[c, i_from]
        return remote(src, meta.at[c, i_to], mt_send.at[c, i_to], mt_recv.at[c, i_to], axis, dist)

    def spread(c, i, step, own, axis):
        for dist in (1, 3, 2):
            ids_copy(c, i, i + dist * step, own, axis, dist).start()
        for dist in (1, 3):
            whole(c, i, i + dist * step, own, axis, dist).start()

    def pass_on(c, dist, i, i_to, axis):
        pl.when(dist == 1)(lambda: top(c, i, i_to, axis).start())
        pl.when(dist == 3)(lambda: bottom(c, i, i_to, axis).start())

    def wait_rows(c, i):
        ids_copy(c, i, i, False, 0, 1).wait_recv()
        whole(c, i, i, False, 0, 1).wait_recv()


    def p_copy(c, d1):
        return remote(mine, packs.at[c, d1 - 1], p_send.at[c, d1 - 1], p_recv.at[c, d1 - 1], _color(c)[0], d1)

    def a_wait(c, i):
        three = ra[c].at[i, pl.ds(0, 3 * cap)]
        pltpu.make_async_copy(three, three, a_recv.at[c, i]).wait()

    def b_copy(c, d1, d2):
        i = d1 * 4 + d2
        return remote(ra[c].at[i], ags[c].at[i], b_send.at[c, i], b_recv.at[c, i], _color(c)[1], _far(d2))

    def forward(k, carry):
        d1, d2 = _order4(k // 4), k % 4
        for c in range(AXES):
            a_wait(c, d1 * 4 + d2)

            @pl.when(d2 > 0)
            def _():
                b_copy(c, d1, d2).start()
        return carry

    def main(st0, st1, st2, wo1, wo3, wo2, xbuf, ring):
        sts, w_own = (st0, st1, st2), (wo1, wo3, wo2)
        w_loads = [pltpu.make_async_copy(w_refs[i], w_own[i], w_loc.at[i]) for i in range(3)]

        def block_copy(c, i, pos, d3):
            off, w = parts[c]
            a1, a2, a3 = _color(c)
            at = [0, 0, 0]
            at[a1], at[a2], at[a3] = i // 4, i % 4, d3
            part = sts[c].at[pos % st_n, pl.ds(d3 * cap, cap)]
            src = at[0] + N_AX * at[1] + N_AX**2 * at[2]
            dst = rows_ref.at[pl.ds(pl.multiple_of(src * cap, cap), cap), pl.ds(off, w)]
            if d3 == 0:
                return pltpu.make_async_copy(part, dst, loc_sem.at[c, pos % st_n])
            return remote(part, dst, blk_send.at[c, pos % st_n, d3 - 1], blk_recv.at[c, at[1] + N_AX * at[2]], a3, d3)

        def pick(c, i, pos, own):
            _, _, a3 = _color(c)
            off, w = parts[c]
            ids = idx_ref[...] if own else meta[c, i]
            member = [jnp.max((ids == _shift(m, {a3: d3})).astype(F32), axis=0, keepdims=True) for d3 in range(N_AX)]
            table = jnp.concatenate(member + [jnp.zeros((4, t_loc), F32)], axis=0)
            slots = jnp.dot(table.astype(BF), tri[...], preferred_element_type=F32)
            key = jnp.where(table > 0, slots, -1.0)
            want = lax.broadcasted_iota(jnp.int32, (cap, t_loc), 0).astype(F32)
            one_hot = jnp.concatenate([jnp.where(key[d3:d3 + 1] == want, 1.0, 0.0) for d3 in range(N_AX)], axis=0)
            one_hot = one_hot.astype(BF)
            for lo in range(0, w, 256):
                hi = min(lo + 256, w)
                xs = x_ref[:, off + lo:off + hi] if own else ags[c][i, :, lo:hi]
                sts[c][pos % st_n, :, lo:hi] = jnp.dot(one_hot, xs, preferred_element_type=F32).astype(BF)

        def local_wait(pos):
            for c in range(AXES):
                block_copy(c, 0, pos, 0).wait()

        def sent_wait(pos):
            for c in range(AXES):
                for d3 in range(1, N_AX):
                    block_copy(c, 0, pos, d3).wait_send()

        def process(i, pos, own=False):
            pl.when(pos >= st_n)(lambda: sent_wait(pos))
            for c in range(AXES):
                pick(c, i, pos, own)
                for d3 in (1, 3, 2, 0):
                    block_copy(c, i, pos, d3).start()
            pl.when(pos >= 1)(lambda: local_wait(pos + st_n - 1))

        r = lax.broadcasted_iota(jnp.int32, (t_loc, t_loc), 0)
        q = lax.broadcasted_iota(jnp.int32, (t_loc, t_loc), 1)
        tri[...] = jnp.where(r < q, 1.0, 0.0).astype(BF)
        for cp in w_loads:
            cp.start()
        _meet()
        for c in range(AXES):
            a1, a2, _ = _color(c)
            spread(c, 0, 4, True, a1)
            spread(c, 0, 1, True, a2)
        for cp in w_swaps:
            cp.start()
        process(0, 0, True)
        mine[...] = _pack(idx_ref, g_ref, n_exp)

        def first_near(k, carry):
            d1 = 1 + 2 * k
            for c in range(AXES):
                a1, a2, _ = _color(c)
                wait_rows(c, d1 * 4)
                pass_on(c, d1, d1 * 4, 8, a1)
                spread(c, d1 * 4, 1, False, a2)
            process(d1 * 4, 1 + k)
            return carry

        def second_near(k, carry):
            d1, d2 = _line(k // 2), 1 + 2 * (k % 2)
            for c in range(AXES):
                wait_rows(c, d1 * 4 + d2)
                pass_on(c, d2, d1 * 4 + d2, d1 * 4 + 2, _color(c)[1])
            process(d1 * 4 + d2, 3 + k + (k + 6) // 8)
            return carry

        def second_far(k, carry):
            d1 = _line(k)
            for c in range(AXES):
                wait_rows(c, d1 * 4 + 2)
            process(d1 * 4 + 2, 12 + k)
            return carry

        lax.fori_loop(0, 2, first_near, 0)
        lax.fori_loop(0, 2, second_near, 0)
        for c in range(AXES):
            wait_rows(c, 8)
            spread(c, 8, 1, False, _color(c)[1])
        process(8, 5)
        lax.fori_loop(2, 8, second_near, 0)
        for c in range(AXES):
            for d1 in (1, 3, 2):
                p_copy(c, d1).start()

        def group_of(n):
            late = n // 12
            near = n % 3
            return (1 - late) * (near + near // 2) + 2 * late, _line((1 - late) * (n // 3) + late * (n - 12))

        def x_copy(n):
            dy, dz = group_of(n)
            return pltpu.make_async_copy(rows_ref.at[pl.ds((dy + N_AX * dz) * blk, blk)], xbuf.at[n % 2], x_sem.at[n % 2])

        def rows_in(n):
            dy, dz = group_of(n)
            g = dy + N_AX * dz

            def arrived(c, count):
                off, w = parts[c]
                ref = rows_ref.at[pl.ds(g * blk, count * cap), pl.ds(off, w)]
                pltpu.make_async_copy(ref, ref, blk_recv.at[c, g]).wait()

            arrived(0, 3)
            pl.when(dy > 0)(lambda: arrived(1, 4))
            pl.when(dz > 0)(lambda: arrived(2, 4))
            x_copy(n).start()

        def a_each(n, far, near):
            dy, dz = group_of(n)
            for c in range(AXES):
                a1, a2, a3 = _color(c)
                off, w = parts[c]
                for dx in range(N_AX):
                    at = (dx, dy, dz)
                    i, d3 = at[a1] * 4 + at[a2], at[a3]

                    def go(c=c, dx=dx, i=i, d3=d3, off=off, w=w, a3=a3):
                        far(remote(ring.at[n % ring_n, pl.ds(dx * cap, cap), pl.ds(off, w)],
                                   ra[c].at[i, pl.ds(d3 * cap, cap)], a_send.at[n % ring_n, c * 4 + dx],
                                   a_recv.at[c, i], a3, _far(d3)))

                    if c == 0:
                        go() if dx else near(c, dx, i)
                    else:
                        pl.when(d3 > 0)(go)
                        pl.when(d3 == 0)(lambda c=c, dx=dx, i=i: near(c, dx, i))

        def step(n, carry):
            x_copy(n).wait()
            pl.when(n + 1 < groups)(lambda: rows_in(n + 1))

            @pl.when(n >= ring_n)
            def _():
                a_each(n - ring_n, lambda cp: cp.wait_send(), lambda c, dx, i: None)

            x = xbuf[n % 2]
            hs = []
            for w1, w3, _ in (w_own, w_parts):
                a = jnp.dot(x, w1[...], preferred_element_type=F32)
                b = jnp.dot(x, w3[...], preferred_element_type=F32)
                hs.append((jax.nn.silu(a) * b).astype(BF))
            for lo in range(0, d, 512):
                y = sum(jnp.dot(h, w[2][:, lo:lo + 512], preferred_element_type=F32) for h, w in zip(hs, (w_own, w_parts)))
                ring[n % ring_n, :, lo:lo + 512] = y.astype(BF)

            def keep(c, dx, i):
                off, w = parts[c]
                ra[c][i, 0:cap, :] = ring[n % ring_n, dx * cap:(dx + 1) * cap, off:off + w]

            a_each(n, lambda cp: cp.start(), keep)
            return carry

        lax.fori_loop(0, N_AX, second_far, 0)
        local_wait(15)
        for cp in w_loads:
            cp.wait()
        for cp in w_swaps:
            cp.wait_recv()
        rows_in(0)

        def drain_far(c, i):
            top(c, i, i, 0).wait_send()
            bottom(c, i, i, 0).wait_send()

        def drain_line(d1, carry):
            for c in range(AXES):
                for d2 in range(1, N_AX):
                    ids_copy(c, 0, d1 * 4 + d2, False, 0, 1).wait_send()
                for d2 in (1, 3):
                    whole(c, 0, d1 * 4 + d2, False, 0, 1).wait_send()
                drain_far(c, d1 * 4 + 2)
            return carry

        lax.fori_loop(0, N_AX, drain_line, 0)
        for c in range(AXES):
            for d1 in range(1, N_AX):
                ids_copy(c, 0, d1 * 4, False, 0, 1).wait_send()
            for d1 in (1, 3):
                whole(c, 0, d1 * 4, False, 0, 1).wait_send()
            drain_far(c, 8)
        for a in range(AXES):
            for dist in range(1, N_AX):
                pl.semaphore_signal(free_sem, inc=1, device_id={"ep": _shift(m, {a: dist})}, device_id_type=MESH)

        lax.fori_loop(0, groups, step, 0)
        pl.semaphore_wait(free_sem, AXES * (N_AX - 1))
        lax.fori_loop(0, groups, forward, 0)

        def drain_ring(n, carry):
            a_each(n, lambda cp: cp.wait_send(), lambda c, dx, i: None)
            return carry

        lax.fori_loop(groups - ring_n, groups, drain_ring, 0)
        for pos in range(16 - st_n, 16):
            sent_wait(pos)
        for cp in w_swaps:
            cp.wait_send()

    weight_scratch = [pltpu.VMEM(w.shape, BF) for w in w_refs]
    pl.run_scoped(main, *[pltpu.VMEM((st_n, blk, w), BF) for _, w in parts], *weight_scratch, pltpu.VMEM((2, blk, d), BF),
                  pltpu.VMEM((ring_n, blk, d), BF))

    def combine(acc, yv, cs0, cs1, cs2, cv0, cv1, cv2):
        cs, cv = (cs0, cs1, cs2), (cv0, cv1, cv2)

        def add_sum(c, d1, d2, own, data):
            _, a2, a3 = _color(c)
            off, w = parts[c]
            table = mine[...] if own else packs[c, d1 - 1]
            row = lax.broadcasted_iota(jnp.int32, (N_AX * n_exp, blk), 0)
            col = lax.broadcasted_iota(jnp.int32, (N_AX * n_exp, blk), 1)
            slot = (lax.broadcasted_iota(jnp.int32, (t_loc, blk), 1) % cap).astype(F32)
            e = _shift(m, {a2: d2}) - m[a3] * N_AX**a3 + ((m[a3] + col // cap) % N_AX) * N_AX**a3
            wide = [jnp.where(row == e + n_exp * k, 1.0, 0.0).astype(BF) for k in range(4)]
            hit = jnp.dot(table, wide[0], preferred_element_type=F32) == slot
            gates = [jnp.where(hit, jnp.dot(table, wide[k], preferred_element_type=F32), 0.0).astype(BF) for k in (1, 2, 3)]
            for lo in range(0, w, 256):
                hi = min(lo + 256, w)
                rows = data[:, lo:hi]
                v = sum(jnp.dot(gate, rows, preferred_element_type=F32) for gate in gates)
                at = acc.at[:, off + lo:off + hi] if own else cs[c].at[d1 - 1, :, lo:hi]
                at[...] = v if data_first(d2) else at[...] + v

        def data_first(d2):
            return isinstance(d2, int)

        def partial_sum(c, d1, own):
            add_sum(c, d1, 0, own, ra[c].at[d1 * 4])

            def more(d2, carry):
                b_copy(c, d1, d2).wait_recv()
                add_sum(c, d1, d2, own, ags[c].at[d1 * 4 + d2])
                return carry

            lax.fori_loop(1, N_AX, more, 0)

        def c_copy(c, d1):
            return remote(cs[c].at[d1 - 1], cr[c].at[d1 - 1], c_send.at[c, d1 - 1], c_recv.at[c, d1 - 1], _color(c)[0],
                          _far(d1))

        for c in range(AXES):
            for d1 in range(1, N_AX):
                p_copy(c, d1).wait_recv()

        def send(k, carry):
            d1 = _order(k)
            for c in range(AXES):
                partial_sum(c, d1, False)
                c_copy(c, d1).start()
            return carry

        lax.fori_loop(0, N_AX - 1, send, 0)
        for c in range(AXES):
            partial_sum(c, 0, True)

        def load(c, d1):
            return pltpu.make_async_copy(cr[c].at[d1 - 1], cv[c].at[d1 - 1], cr_sem.at[c, d1 - 1])

        def store(c):
            off, w = parts[c]
            return pltpu.make_async_copy(yv.at[:, pl.ds(off, w)], y_ref.at[:, pl.ds(off, w)], w_loc.at[c])

        for d1 in (1, 3, 2):
            for c in range(AXES):
                c_copy(c, d1).wait()
                load(c, d1).start()
        for c in range(AXES):
            off, w = parts[c]
            for d1 in (1, 3, 2):
                load(c, d1).wait()
            yv[:, off:off + w] = (acc[:, off:off + w] + cv[c][0] + cv[c][1] + cv[c][2]).astype(BF)
            store(c).start()
        for c in range(AXES):
            store(c).wait()

    pl.run_scoped(combine, pltpu.VMEM((t_loc, d), F32), pltpu.VMEM((t_loc, d), BF), *[pltpu.VMEM((3, t_loc, w), F32) for _, w in parts],
                  *[pltpu.VMEM((3, t_loc, w), F32) for _, w in parts])

    def drain_b(k, carry):
        for c in range(AXES):
            for d2 in range(1, N_AX):
                b_copy(c, k, d2).wait_send()
        return carry

    lax.fori_loop(0, N_AX, drain_b, 0)
    for c in range(AXES):
        for d1 in range(1, N_AX):
            p_copy(c, d1).wait_send()


def _layer(x, idx, g, w1, w3, w2, cap):
    t_loc, d = x.shape
    parts = _parts(d)
    blk = N_AX * cap
    ring_n, st_n = 4, 3
    n_exp = N_AX**AXES
    any_spec = pl.BlockSpec(memory_space=pl.ANY)
    vm = pl.BlockSpec(memory_space=pltpu.VMEM)
    dma = pltpu.SemaphoreType.DMA
    return pl.pallas_call(
        functools.partial(_layer_kernel, parts, cap, ring_n, st_n),
        out_shape=[jax.ShapeDtypeStruct((t_loc, d), BF), jax.ShapeDtypeStruct((n_exp * cap, d), BF)]
        + [jax.ShapeDtypeStruct((3, t_loc, w), F32) for _, w in parts],
        in_specs=[vm, vm, vm] + [any_spec] * 3,
        out_specs=[any_spec] * 5,
        scratch_shapes=[pltpu.VMEM((16, blk, w), BF) for _, w in parts]
        + [pltpu.VMEM((16, blk, w), BF) for _, w in parts]
        + [pltpu.VMEM(w.shape, BF) for w in (w1, w3, w2)]
        + [pltpu.VMEM((3, 16) + idx.shape, jnp.int32), pltpu.VMEM((3, 3, t_loc, 4 * n_exp), BF),
           pltpu.VMEM((t_loc, 4 * n_exp), BF), pltpu.VMEM((t_loc, t_loc), BF),
           dma((3, 16)), dma((3, 16)), dma((3, 16)), dma((3, 16)), dma((3, 16)), dma((3, st_n, 3)), dma((3, 16)),
           dma((3, st_n)), dma((3,)), dma((3,)), dma((3,)), dma((2,)), dma((ring_n, 12)), dma((3, 16)), dma((3, 16)),
           dma((3, 16)), dma((3, 3)), dma((3, 3)), dma((3, 3)), dma((3, 3)), dma((3, 3)), pltpu.SemaphoreType.REGULAR],
        compiler_params=pltpu.CompilerParams(collective_id=0, has_side_effects=True, vmem_limit_bytes=67_043_328),
        name="layer",
    )(x, idx, g, w1, w3, w2)[0]


def solution(mesh):
    ep = mesh.shape["ep"]
    rows = P(("dp", "ep", "tp"), None)

    def local(x, idx, g, w1, w3, w2):
        cap = CF * idx.shape[1] * x.shape[0] // ep
        return _layer(x, idx.T, g.T, w1[0], w3[0], w2[0], cap)

    return jax.shard_map(local, mesh=mesh,
                         in_specs=(rows, rows, rows, P("ep", None, "tp"), P("ep", None, "tp"), P("ep", "tp", None)),
                         out_specs=rows, check_vma=False)
```

time: 836 us -> 315 us (0.38); the launches traced: 823 us -> 314 us
  waiting for transfers between devices: 331 us -> 0 us
  Pallas kernels: 0 us -> 312 us
  blocking collectives: 296 us -> 0 us
  matrix products: 70 us -> 0 us
  other arithmetic: 53.2 us -> 0 us
  local copies, waits for them, and re-layouts: 49.2 us -> 2.3 us
  between operations: 13.7 us -> 0.01 us
  starting transfers between devices: 10.8 us -> 0 us
    pallas_call x0 -> x1, Pallas kernels: none -> 312 us  [_layer(): pl.pallas_call(functools.partial(_layer_kernel, parts, cap, ring_n, st_n)...]
    all_to_all x2 -> x0, blocking collectives: 296 us -> none  [the longest x1 226 us: local(): recv = lax.all_to_all(buf, 'ep', 0, 0, tiled=True)]
    all_to_all x1 -> x0, waiting for transfers between devices: 273 us -> none  [local(): back = lax.all_to_all(y, 'ep', 0, 0, tiled=True).reshape(n_exp * cap, d)]
    dot_general x2 -> x0, matrix products: 70 us -> none  [the longest x1 44.6 us: local(): jnp.einsum('erf,efd->erd', h, w2, preferred_element_type=jnp.float32)]
    all_gather x1 -> x0, waiting for transfers between devices: 57.6 us -> none  [local(): allr = lax.all_gather(recv, 'tp', axis=0)]
    reduce_sum x3 -> x0, other arithmetic: 33.3 us -> none  [the longest x1 20.8 us: local(): y = jnp.sum(parts.astype(jnp.float32), axis=0).astype(jnp.bfloat16)]
    gather x1 -> x0, local copies, waits for them, and re-layouts: 24.4 us -> none  [local(): back[jnp.minimum(dest, n_exp * cap - 1)].astype(jnp.float32)]
    scatter x1 -> x0, local copies, waits for them, and re-layouts: 21.9 us -> none  [local(): jnp.zeros((n_exp * cap, d), x.dtype).at[dest].set(xr, mode='drop')]
  transfers between devices with their start and end apart: 2 -> 0, of which waited for: 2 -> 0; matrix products, arithmetic and copies ran while one was open for 0% -> 0% of each run, Pallas kernels for 0% -> 0%
where the time goes in v4:
time: 315 us; the launch traced here: 314 us
  Pallas kernels  312 us (99%)
    pallas_call x1, Pallas kernels, _layer(): pl.pallas_call(functools.partial(_layer_kernel, parts, cap, ring_n, st_n)...  312 us

profile of v4, /device:TPU:0, one launch (start us, length us, event | category | flops | bytes accessed | tf_op | source)
XLA Modules:
  0.0 314.4 jit_solution(3505689783413376202)
XLA Ops:
  0.0 312.1 %layer.1 = (bf16[256,2048]{1,0:T(8,128)(2,1)}, bf16[4096,2048]{1,0:T(8,128)(2,1)}, f32[3,256,768]{2,1,0:T(8,128)}, f32[3,256,640]{2,1,0:T(8,128)}, f32[3,256,640]{2,1,0:T(8,128)}) custom-call(bf16[256,2048]{1,0:T(8,128)(2,1)} %x_ref.1, s32[8,256]{1,0:T(8,128)} %bitcast.8, f32[8,256]{1,0:T(8,128)} %bitcast.9, bf16[2048,512]{1,0:T(8,128)(2,1)} %bitcast.5, ...), custom_call_target="tpu_custom_call" | custom-call | tf_op jit(solution)/shard_map/layer/pallas_call | solution.py:479
  312.1 2.3 copy.8

commit v5 on v4

--- a/solution.py
+++ b/solution.py
@@ -42,10 +42,6 @@
 
 def _line(k):
     return k + k // 2 - 2 * (k // 3)
-
-
-def _order(k):
-    return 1 + 2 * k - 3 * (k // 2)
 
 
 def _split3(v):
@@ -77,6 +73,10 @@
     return N_AX - d
 
 
+def _order(k):
+    return 1 + 2 * k - 3 * (k // 2)
+
+
 def _order4(k):
     return (1 + 2 * k - 3 * (k // 2)) % N_AX
 
@@ -86,12 +86,13 @@
 
 
 def _layer_kernel(parts, cap, ring_n, st_n, x_ref, idx_ref, g_ref, w1_ref, w3_ref, w2_ref, y_ref, rows_ref, cr0, cr1, cr2,
-                  ag0, ag1, ag2, ra0, ra1, ra2, wp1, wp3, wp2, meta, packs, mine, tri, *sems):
+                  ag0, ag1, ag2, ra0, ra1, ra2, wp1, wp3, wp2, meta, gates_in, packs, mine, tri, *sems):
     (ag_send, ag_send2, ag_recv, mt_send, mt_recv, blk_send, blk_recv, loc_sem, w_send, w_recv, w_loc, x_sem, a_send, a_recv,
-     b_send, b_recv, c_send, c_recv, cr_sem, p_send, p_recv, free_sem) = sems
+     b_send, b_recv, c_send, c_recv, cr_sem, g_send, g_recv, free_sem) = sems
     me, tp = lax.axis_index("ep"), lax.axis_index("tp")
     m = _coords(me)
     ags, ra, cr = (ag0, ag1, ag2), (ra0, ra1, ra2), (cr0, cr1, cr2)
+    back, rb = parts, ags
     t_loc, d = x_ref.shape
     n_exp = N_AX**AXES
     half = t_loc // 2
@@ -140,8 +141,8 @@
         whole(c, i, i, False, 0, 1).wait_recv()
 
 
-    def p_copy(c, d1):
-        return remote(mine, packs.at[c, d1 - 1], p_send.at[c, d1 - 1], p_recv.at[c, d1 - 1], _color(c)[0], d1)
+    def g_copy(c, d1):
+        return remote(g_ref, gates_in.at[c, d1 - 1], g_send.at[c, d1 - 1], g_recv.at[c, d1 - 1], _color(c)[0], d1)
 
     def a_wait(c, i):
         three = ra[c].at[i, pl.ds(0, 3 * cap)]
@@ -149,7 +150,7 @@
 
     def b_copy(c, d1, d2):
         i = d1 * 4 + d2
-        return remote(ra[c].at[i], ags[c].at[i], b_send.at[c, i], b_recv.at[c, i], _color(c)[1], _far(d2))
+        return remote(ra[c].at[i], rb[c].at[i], b_send.at[c, i], b_recv.at[c, i], _color(c)[1], _far(d2))
 
     def forward(k, carry):
         d1, d2 = _order4(k // 4), k % 4
@@ -220,6 +221,8 @@
             a1, a2, _ = _color(c)
             spread(c, 0, 4, True, a1)
             spread(c, 0, 1, True, a2)
+            for d1 in (1, 3, 2):
+                g_copy(c, d1).start()
         for cp in w_swaps:
             cp.start()
         process(0, 0, True)
@@ -257,9 +260,6 @@
             spread(c, 8, 1, False, _color(c)[1])
         process(8, 5)
         lax.fori_loop(2, 8, second_near, 0)
-        for c in range(AXES):
-            for d1 in (1, 3, 2):
-                p_copy(c, d1).start()
 
         def group_of(n):
             late = n // 12
@@ -288,7 +288,7 @@
             dy, dz = group_of(n)
             for c in range(AXES):
                 a1, a2, a3 = _color(c)
-                off, w = parts[c]
+                off, w = back[c]
                 for dx in range(N_AX):
                     at = (dx, dy, dz)
                     i, d3 = at[a1] * 4 + at[a2], at[a3]
@@ -323,19 +323,23 @@
                 ring[n % ring_n, :, lo:lo + 512] = y.astype(BF)
 
             def keep(c, dx, i):
-                off, w = parts[c]
+                off, w = back[c]
                 ra[c][i, 0:cap, :] = ring[n % ring_n, dx * cap:(dx + 1) * cap, off:off + w]
 
             a_each(n, lambda cp: cp.start(), keep)
             return carry
 
-        lax.fori_loop(0, N_AX, second_far, 0)
-        local_wait(15)
         for cp in w_loads:
             cp.wait()
         for cp in w_swaps:
             cp.wait_recv()
-        rows_in(0)
+        def last_rounds(k, carry):
+            second_far(k, 0)
+            pl.when(k == 1)(lambda: rows_in(0))
+            pl.when(k == 3)(lambda: local_wait(15))
+            return lax.fori_loop(2 * (k - (k + 3) // 4), 2 * k + 10 * (k // 3), step, carry)
+
+        lax.fori_loop(0, N_AX, last_rounds, 0)
 
         def drain_far(c, i):
             top(c, i, i, 0).wait_send()
@@ -361,9 +365,16 @@
             for dist in range(1, N_AX):
                 pl.semaphore_signal(free_sem, inc=1, device_id={"ep": _shift(m, {a: dist})}, device_id_type=MESH)
 
-        lax.fori_loop(0, groups, step, 0)
         pl.semaphore_wait(free_sem, AXES * (N_AX - 1))
         lax.fori_loop(0, groups, forward, 0)
+
+        def unpack(k, carry):
+            for c in range(AXES):
+                g_copy(c, k + 1).wait_recv()
+                packs[c, k] = _pack(meta.at[c, (k + 1) * 4], gates_in.at[c, k], n_exp)
+            return carry
+
+        lax.fori_loop(0, N_AX - 1, unpack, 0)
 
         def drain_ring(n, carry):
             a_each(n, lambda cp: cp.wait_send(), lambda c, dx, i: None)
@@ -384,7 +395,7 @@
 
         def add_sum(c, d1, d2, own, data):
             _, a2, a3 = _color(c)
-            off, w = parts[c]
+            off, w = back[c]
             table = mine[...] if own else packs[c, d1 - 1]
             row = lax.broadcasted_iota(jnp.int32, (N_AX * n_exp, blk), 0)
             col = lax.broadcasted_iota(jnp.int32, (N_AX * n_exp, blk), 1)
@@ -408,7 +419,7 @@
 
             def more(d2, carry):
                 b_copy(c, d1, d2).wait_recv()
-                add_sum(c, d1, d2, own, ags[c].at[d1 * 4 + d2])
+                add_sum(c, d1, d2, own, rb[c].at[d1 * 4 + d2])
                 return carry
 
             lax.fori_loop(1, N_AX, more, 0)
@@ -417,9 +428,12 @@
             return remote(cs[c].at[d1 - 1], cr[c].at[d1 - 1], c_send.at[c, d1 - 1], c_recv.at[c, d1 - 1], _color(c)[0],
                           _far(d1))
 
-        for c in range(AXES):
-            for d1 in range(1, N_AX):
-                p_copy(c, d1).wait_recv()
+        def load(c, d1):
+            return pltpu.make_async_copy(cr[c].at[d1 - 1], cv[c].at[d1 - 1], cr_sem.at[c, d1 - 1])
+
+        def store(c):
+            off, w = back[c]
+            return pltpu.make_async_copy(yv.at[:, pl.ds(off, w)], y_ref.at[:, pl.ds(off, w)], w_loc.at[c])
 
         def send(k, carry):
             d1 = _order(k)
@@ -431,29 +445,23 @@
         lax.fori_loop(0, N_AX - 1, send, 0)
         for c in range(AXES):
             partial_sum(c, 0, True)
-
-        def load(c, d1):
-            return pltpu.make_async_copy(cr[c].at[d1 - 1], cv[c].at[d1 - 1], cr_sem.at[c, d1 - 1])
-
-        def store(c):
-            off, w = parts[c]
-            return pltpu.make_async_copy(yv.at[:, pl.ds(off, w)], y_ref.at[:, pl.ds(off, w)], w_loc.at[c])
-
         for d1 in (1, 3, 2):
             for c in range(AXES):
-                c_copy(c, d1).wait()
+                c_copy(c, d1).wait_recv()
                 load(c, d1).start()
         for c in range(AXES):
-            off, w = parts[c]
+            off, w = back[c]
             for d1 in (1, 3, 2):
                 load(c, d1).wait()
             yv[:, off:off + w] = (acc[:, off:off + w] + cv[c][0] + cv[c][1] + cv[c][2]).astype(BF)
             store(c).start()
         for c in range(AXES):
             store(c).wait()
-
-    pl.run_scoped(combine, pltpu.VMEM((t_loc, d), F32), pltpu.VMEM((t_loc, d), BF), *[pltpu.VMEM((3, t_loc, w), F32) for _, w in parts],
-                  *[pltpu.VMEM((3, t_loc, w), F32) for _, w in parts])
+            for d1 in (1, 3, 2):
+                c_copy(c, d1).wait_send()
+
+    pl.run_scoped(combine, pltpu.VMEM((t_loc, d), F32), pltpu.VMEM((t_loc, d), BF), *[pltpu.VMEM((3, t_loc, w), F32) for _, w in back],
+                  *[pltpu.VMEM((3, t_loc, w), F32) for _, w in back])
 
     def drain_b(k, carry):
         for c in range(AXES):
@@ -464,7 +472,7 @@
     lax.fori_loop(0, N_AX, drain_b, 0)
     for c in range(AXES):
         for d1 in range(1, N_AX):
-            p_copy(c, d1).wait_send()
+            g_copy(c, d1).wait_send()
 
 
 def _layer(x, idx, g, w1, w3, w2, cap):
@@ -485,7 +493,7 @@
         scratch_shapes=[pltpu.VMEM((16, blk, w), BF) for _, w in parts]
         + [pltpu.VMEM((16, blk, w), BF) for _, w in parts]
         + [pltpu.VMEM(w.shape, BF) for w in (w1, w3, w2)]
-        + [pltpu.VMEM((3, 16) + idx.shape, jnp.int32), pltpu.VMEM((3, 3, t_loc, 4 * n_exp), BF),
+        + [pltpu.VMEM((3, 16) + idx.shape, jnp.int32), pltpu.VMEM((3, 3) + g.shape, F32), pltpu.VMEM((3, 3, t_loc, 4 * n_exp), BF),
            pltpu.VMEM((t_loc, 4 * n_exp), BF), pltpu.VMEM((t_loc, t_loc), BF),
            dma((3, 16)), dma((3, 16)), dma((3, 16)), dma((3, 16)), dma((3, 16)), dma((3, st_n, 3)), dma((3, 16)),
            dma((3, st_n)), dma((3,)), dma((3,)), dma((3,)), dma((2,)), dma((ring_n, 12)), dma((3, 16)), dma((3, 16)),

time: 315 us -> 306 us (0.971)
  Pallas kernels: 312 us -> 304 us
    pallas_call x1, Pallas kernels: 312 us -> 304 us  [_layer(): pl.pallas_call(functools.partial(_layer_kernel, parts, cap, ring_n, st_n)...]
where the time goes in v5:
time: 306 us
  Pallas kernels  304 us (99%)
    pallas_call x1, Pallas kernels, _layer(): pl.pallas_call(functools.partial(_layer_kernel, parts, cap, ring_n, st_n)...  304 us

profile of v5, /device:TPU:0, one launch (start us, length us, event | category | flops | bytes accessed | tf_op | source)
XLA Modules:
  0.0 305.9 jit_solution(18271281370798124395)
XLA Ops:
  0.0 303.6 %layer.1 = (bf16[256,2048]{1,0:T(8,128)(2,1)}, bf16[4096,2048]{1,0:T(8,128)(2,1)}, f32[3,256,768]{2,1,0:T(8,128)}, f32[3,256,640]{2,1,0:T(8,128)}, f32[3,256,640]{2,1,0:T(8,128)}) custom-call(bf16[256,2048]{1,0:T(8,128)(2,1)} %x_ref.1, s32[8,256]{1,0:T(8,128)} %bitcast.8, f32[8,256]{1,0:T(8,128)} %bitcast.9, bf16[2048,512]{1,0:T(8,128)(2,1)} %bitcast.5, ...), custom_call_target="tpu_custom_call" | custom-call | tf_op jit(solution)/shard_map/layer/pallas_call | solution.py:487
  303.6 2.3 copy.8
